TPU v7x, 8 devices: a whole 2x2x1 slice. The times are simulated.
8 devices in a mesh: data: 8 (over z, y, x, core).
Axes of the slice: x: 2, y: 2, z: 1, core: 2. Of those that a mesh axis runs over, the one named last changes fastest.
Arguments:
- x_in: bfloat16 [48, 384, 512], P('data')
- g_out: bfloat16 [48, 384, 512], P('data')
- step_emb: bfloat16 [3, 512], replicated
- w_q: bfloat16 [512, 8, 64], replicated
- w_k: bfloat16 [512, 8, 64], replicated
- w_v: bfloat16 [512, 8, 64], replicated
- w_o: bfloat16 [8, 64, 512], replicated
- w_up: bfloat16 [512, 2048], replicated
- w_down: bfloat16 [2048, 512], replicated
Outputs:
- output 1: float32 [512, 8, 64], replicated
- output 2: float32 [512, 8, 64], replicated
- output 3: float32 [512, 8, 64], replicated
- output 4: float32 [8, 64, 512], replicated
- output 5: float32 [512, 2048], replicated
- output 6: float32 [2048, 512], replicated
- output 7: bfloat16 [48, 384, 512], P('data')
All inputs are finite; a program needn't handle non-finite values.
Results may differ from a plain program's by a relative error of at most 0.02.
Values are sent between devices in bfloat16 or wider.
A program may use at most 1 GiB of HBM per device.

v0:
```python
import jax
import jax.numpy as jnp
from jax import lax
from jax.sharding import PartitionSpec as P, NamedSharding
import functools

NORM_EPS = 1e-6


def rms_norm(x_val):
    x_f32 = x_val.astype(jnp.float32)
    return (x_f32 * lax.rsqrt(jnp.mean(x_f32 * x_f32, axis=-1, keepdims=True) + NORM_EPS)).astype(jnp.bfloat16)


def gelu_act(z_val):
    return jax.nn.gelu(z_val.astype(jnp.float32), approximate=True).astype(jnp.bfloat16)


def attn_probs(scores, attn_scale):
    return jax.nn.softmax(scores.astype(jnp.float32) * attn_scale, axis=-1).astype(jnp.bfloat16)


def layer_fwd(x_prev, step_vec, weight_set, attn_scale):
    w_qkv, w_o, w_up, w_down = weight_set
    n_heads = w_o.shape[0]
    x_cur = x_prev + step_vec
    u_norm = rms_norm(x_cur)
    qkv_heads = jnp.einsum('bsd,dhe->bshe', u_norm, w_qkv, preferred_element_type=jnp.float32).astype(jnp.bfloat16)
    q_heads = qkv_heads[:, :, :n_heads]
    k_heads = qkv_heads[:, :, n_heads:2 * n_heads]
    v_heads = qkv_heads[:, :, 2 * n_heads:]
    scores = jnp.einsum('bqhe,bkhe->bhqk', q_heads, k_heads, preferred_element_type=jnp.float32).astype(jnp.bfloat16)
    prob_mat = attn_probs(scores, attn_scale)
    mix_heads = jnp.einsum('bhqk,bkhe->bqhe', prob_mat, v_heads, preferred_element_type=jnp.float32).astype(jnp.bfloat16)
    attn_out = jnp.einsum('crif,ife->cre', mix_heads, w_o, preferred_element_type=jnp.float32).astype(jnp.bfloat16)
    h_mid = x_cur + attn_out
    z_up = jnp.dot(rms_norm(h_mid), w_up, preferred_element_type=jnp.float32).astype(jnp.bfloat16)
    y_down = jnp.dot(gelu_act(z_up), w_down, preferred_element_type=jnp.float32).astype(jnp.bfloat16)
    return h_mid + y_down, (x_cur, qkv_heads, mix_heads, h_mid, z_up)


def layer_bwd(d_out, saved_acts, weight_set, attn_scale):
    w_qkv, w_o, w_up, w_down = weight_set
    x_cur, qkv_heads, mix_heads, h_mid, z_up = saved_acts
    n_heads = w_o.shape[0]
    g_act, gelu_pull = jax.vjp(gelu_act, z_up)
    grad_down = jnp.einsum('bsf,bsd->fd', g_act, d_out, preferred_element_type=jnp.float32)
    d_act = jnp.einsum('bsd,fd->bsf', d_out, w_down, preferred_element_type=jnp.float32).astype(jnp.bfloat16)
    (d_up,) = gelu_pull(d_act)
    m_norm, norm_pull_h = jax.vjp(rms_norm, h_mid)
    grad_up = jnp.einsum('bsd,bsf->df', m_norm, d_up, preferred_element_type=jnp.float32)
    d_norm_h = jnp.einsum('bsf,df->bsd', d_up, w_up, preferred_element_type=jnp.float32).astype(jnp.bfloat16)
    (d_mid_norm,) = norm_pull_h(d_norm_h)
    d_mid = d_out + d_mid_norm
    grad_o = jnp.einsum('crif,cre->ife', mix_heads, d_mid, preferred_element_type=jnp.float32)
    d_mix = jnp.einsum('cre,ife->crif', d_mid, w_o, preferred_element_type=jnp.float32).astype(jnp.bfloat16)
    q_heads = qkv_heads[:, :, :n_heads]
    k_heads = qkv_heads[:, :, n_heads:2 * n_heads]
    v_heads = qkv_heads[:, :, 2 * n_heads:]
    scores = jnp.einsum('bqhe,bkhe->bhqk', q_heads, k_heads, preferred_element_type=jnp.float32).astype(jnp.bfloat16)
    prob_mat, prob_pull = jax.vjp(functools.partial(attn_probs, attn_scale=attn_scale), scores)
    d_v = jnp.einsum('bhqk,bqhe->bkhe', prob_mat, d_mix, preferred_element_type=jnp.float32).astype(jnp.bfloat16)
    d_prob = jnp.einsum('bqhe,bkhe->bhqk', d_mix, v_heads, preferred_element_type=jnp.float32).astype(jnp.bfloat16)
    (d_scores,) = prob_pull(d_prob)
    d_q = jnp.einsum('bhqk,bkhe->bqhe', d_scores, k_heads, preferred_element_type=jnp.float32).astype(jnp.bfloat16)
    d_k = jnp.einsum('bhqk,bqhe->bkhe', d_scores, q_heads, preferred_element_type=jnp.float32).astype(jnp.bfloat16)
    d_qkv = jnp.concatenate([d_q, d_k, d_v], axis=2)
    u_norm, norm_pull_x = jax.vjp(rms_norm, x_cur)
    grad_qkv = jnp.einsum('bsd,bshe->dhe', u_norm, d_qkv, preferred_element_type=jnp.float32)
    d_norm_x = jnp.einsum('bshe,dhe->bsd', d_qkv, w_qkv, preferred_element_type=jnp.float32).astype(jnp.bfloat16)
    (d_cur_norm,) = norm_pull_x(d_norm_x)
    return d_mid + d_cur_norm, (grad_qkv, grad_o, grad_up, grad_down)


def micro_pass(x_mb, g_mb, step_emb, weight_set, attn_scale):
    n_layers = step_emb.shape[0]
    x_cur = x_mb
    saved_list = []
    for layer_idx in range(n_layers):
        x_cur, saved_acts = layer_fwd(x_cur, step_emb[layer_idx], weight_set, attn_scale)
        saved_list.append(saved_acts)
    d_cur = g_mb
    grad_sum = tuple(jnp.zeros(w.shape, jnp.float32) for w in weight_set)
    for layer_idx in reversed(range(n_layers)):
        d_cur, layer_grads = layer_bwd(d_cur, saved_list[layer_idx], weight_set, attn_scale)
        grad_sum = tuple(acc_part + new_part for acc_part, new_part in zip(grad_sum, layer_grads))
    return d_cur, grad_sum


def solution(mesh):
    batch_spec = P('data', None, None)

    def per_device(x_loc, g_loc, step_emb, w_q, w_k, w_v, w_o, w_up, w_down):
        n_heads = w_q.shape[1]
        attn_scale = w_q.shape[2] ** -0.5
        weight_set = (jnp.concatenate([w_q, w_k, w_v], axis=1), w_o, w_up, w_down)
        rows_mb = x_loc.shape[0] // 2
        dx_parts = []
        grad_total = tuple(jnp.zeros(w.shape, jnp.float32) for w in weight_set)
        for micro_idx in range(2):
            start_row = micro_idx * rows_mb
            d_x, micro_grads = micro_pass(x_loc[start_row:start_row + rows_mb], g_loc[start_row:start_row + rows_mb], step_emb, weight_set, attn_scale)
            reduced = lax.psum(micro_grads, 'data')
            grad_total = tuple(acc_part + new_part for acc_part, new_part in zip(grad_total, reduced))
            dx_parts.append(d_x)
        grad_qkv, grad_o, grad_up, grad_down = grad_total
        return (grad_qkv[:, :n_heads], grad_qkv[:, n_heads:2 * n_heads], grad_qkv[:, 2 * n_heads:], grad_o, grad_up, grad_down, jnp.concatenate(dx_parts, axis=0))

    return jax.shard_map(per_device, mesh=mesh, in_specs=(batch_spec, batch_spec, P(), P(), P(), P(), P(), P(), P()), out_specs=(P(), P(), P(), P(), P(), P(), batch_spec), check_vma=False)
```

profile of v0, /device:TPU:0, one launch (start us, length us, event | category | flops | bytes accessed | tf_op | source)
XLA Modules:
  0.0 765.1 jit_solution(13595608893759694498)
XLA Ops:
  20.1 7.3 fusion.442
  28.0 9.7 %divide_convert_fusion.2 = bf16[3,8,384,384]{2,3,1,0:T(8,128)(2,1)} fusion(f32[3,8,384,384]{2,3,1,0:T(8,128)} %get-tuple-element.44, f32[3,8,384]{2,1,0:T(8,128)S(1)} %get-tuple-element.43), kind=kLoop, calls=%fused_computation.86 | loop fusion | flops 7077888 | bytes 21270528 | tf_op jit(solution)/shard_map/convert_element_type | solution.py:20
  66.0 9.7 %divide_convert_fusion.1 = bf16[3,8,384,384]{2,3,1,0:T(8,128)(2,1)} fusion(f32[3,8,384,384]{2,3,1,0:T(8,128)} %get-tuple-element.50, f32[3,8,384]{2,1,0:T(8,128)S(1)} %get-tuple-element.49), kind=kLoop, calls=%fused_computation.82 | loop fusion | flops 7077888 | bytes 21270528 | tf_op jit(solution)/shard_map/convert_element_type | solution.py:20
  96.9 6.9 fusion.444
  104.5 9.6 %divide_convert_fusion = bf16[3,8,384,384]{2,3,1,0:T(8,128)(2,1)} fusion(f32[3,8,384,384]{2,3,1,0:T(8,128)} %get-tuple-element.56, f32[3,8,384]{2,1,0:T(8,128)S(1)} %get-tuple-element.55), kind=kLoop, calls=%fused_computation.78 | loop fusion | flops 7077888 | bytes 21270528 | tf_op jit(solution)/shard_map/convert_element_type | solution.py:20
  128.9 8.9 %fusion.65 = bf16[3,384,2048]{2,1,0:T(8,128)(2,1)S(1)} fusion(bf16[3,384,2048]{2,1,0:T(8,128)(2,1)S(1)} %convolution_convert_fusion.12, bf16[6,384,512]{2,1,0:T(8,128)(2,1)S(1)} %copy-done.32, bf16[2048,512]{1,0:T(8,128)(2,1)S(1)} %copy-done.141), kind=kOutput, calls=%fused_computation.131 | convolution fusion | flops 2470182912 | bytes 13893632 | tf_op jit(solution)/shard_map/bsd,fd->bsf/dot_general | solution.py:48
  161.2 9.6 %divide_convert_fusion.5 = bf16[3,8,384,384]{2,3,1,0:T(8,128)(2,1)} fusion(f32[3,8,384,384]{2,3,1,0:T(8,128)} %get-tuple-element.26, f32[3,8,384]{2,1,0:T(8,128)S(1)} %get-tuple-element.25), kind=kLoop, calls=%fused_computation.98 | loop fusion | flops 7077888 | bytes 21270528 | tf_op jit(solution)/shard_map/convert_element_type | solution.py:20
  191.7 7.1 fusion.440
  199.4 9.6 %divide_convert_fusion.4 = bf16[3,8,384,384]{2,3,1,0:T(8,128)(2,1)} fusion(f32[3,8,384,384]{2,3,1,0:T(8,128)} %get-tuple-element.32, f32[3,8,384]{2,1,0:T(8,128)S(1)} %get-tuple-element.31), kind=kLoop, calls=%fused_computation.94 | loop fusion | flops 7077888 | bytes 21270528 | tf_op jit(solution)/shard_map/convert_element_type | solution.py:20
  230.3 6.9 fusion.441
  237.9 9.6 %divide_convert_fusion.3 = bf16[3,8,384,384]{2,3,1,0:T(8,128)(2,1)} fusion(f32[3,8,384,384]{2,3,1,0:T(8,128)} %get-tuple-element.38, f32[3,8,384]{2,1,0:T(8,128)S(1)} %get-tuple-element.37), kind=kLoop, calls=%fused_computation.90 | loop fusion | flops 7077888 | bytes 21270528 | tf_op jit(solution)/shard_map/convert_element_type | solution.py:20
  256.3 8.5 %fusion.56 = bf16[3,384,2048]{2,1,0:T(8,128)(2,1)S(1)} fusion(bf16[3,384,2048]{2,1,0:T(8,128)(2,1)S(1)} %convolution_convert_fusion.15, bf16[6,384,512]{2,1,0:T(8,128)(2,1)S(1)} %copy-done.33, bf16[2048,512]{1,0:T(8,128)(2,1)S(1)} %copy-done.144), kind=kOutput, calls=%fused_computation.122 | convolution fusion | flops 2470182912 | bytes 13893632 | tf_op jit(solution)/shard_map/bsd,fd->bsf/dot_general | solution.py:48
  278.4 7.7 %fusion.25 = (f32[3,8,384]{2,1,0:T(8,128)S(1)}, bf16[3,8,384,384]{2,3,1,0:T(8,128)(2,1)S(1)}) fusion(f32[3,8,384,384]{2,3,1,0:T(8,128)} %get-tuple-element.56, f32[3,8,384]{2,1,0:T(8,128)S(1)} %copy-done.86, bf16[3,384,8,64]{1,3,2,0:T(8,128)(2,1)S(1)} %convolution_convert_fusion.50, bf16[3,384,24,64]{1,3,2,0:T(8,128)(2,1)} %copy-done.67), kind=kOutput, calls=%fused_computation.67 | convolution fusion | flops 470670336 | bytes 23666688 | tf_op jit(solution)/shard_map/bqhe,bkhe->bhqk/dot_general | solution.py:63
  286.1 7.3 fusion.44
  310.9 8.6 %fusion.68 = bf16[3,384,2048]{2,1,0:T(8,128)(2,1)S(1)} fusion(bf16[3,384,2048]{2,1,0:T(8,128)(2,1)S(1)} %bitcast.562, bf16[3,384,512]{2,1,0:T(8,128)(2,1)S(1)} %fusion.314, bf16[2048,512]{1,0:T(8,128)(2,1)S(1)} %copy-done.145), kind=kOutput, calls=%fused_computation.134 | convolution fusion | flops 2470182912 | bytes 12713984 | tf_op jit(solution)/shard_map/bsd,fd->bsf/dot_general | solution.py:48
  333.6 7.7 %fusion.30 = (f32[3,8,384]{2,1,0:T(8,128)S(1)}, bf16[3,8,384,384]{2,3,1,0:T(8,128)(2,1)S(1)}) fusion(f32[3,8,384,384]{2,3,1,0:T(8,128)} %get-tuple-element.50, f32[3,8,384]{2,1,0:T(8,128)S(1)} %copy-done.84, bf16[3,384,8,64]{1,3,2,0:T(8,128)(2,1)S(1)} %convolution_convert_fusion.49, bf16[3,384,24,64]{1,3,2,0:T(8,128)(2,1)} %copy-done.63), kind=kOutput, calls=%fused_computation.72 | convolution fusion | flops 470670336 | bytes 23666688 | tf_op jit(solution)/shard_map/bqhe,bkhe->bhqk/dot_general | solution.py:63
  341.3 7.2 fusion.43
  365.6 8.9 %fusion.71 = bf16[3,384,2048]{2,1,0:T(8,128)(2,1)S(1)} fusion(bf16[3,384,2048]{2,1,0:T(8,128)(2,1)S(1)} %bitcast.558, bf16[3,384,512]{2,1,0:T(8,128)(2,1)S(1)} %fusion.312, bf16[2048,512]{1,0:T(8,128)(2,1)S(1)} %copy-done.146), kind=kOutput, calls=%fused_computation.137 | convolution fusion | flops 2470182912 | bytes 12713984 | tf_op jit(solution)/shard_map/bsd,fd->bsf/dot_general | solution.py:48
  385.3 7.7 fusion.35
  392.9 7.1 fusion.42
  409.7 7.7 %fusion.10 = (f32[3,8,384]{2,1,0:T(8,128)S(1)}, bf16[3,8,384,384]{2,3,1,0:T(8,128)(2,1)S(1)}) fusion(f32[3,8,384,384]{2,3,1,0:T(8,128)} %get-tuple-element.38, f32[3,8,384]{2,1,0:T(8,128)S(1)} %copy-done.85, bf16[3,384,8,64]{1,3,2,0:T(8,128)(2,1)S(1)} %convolution_convert_fusion.53, bf16[3,384,24,64]{1,3,2,0:T(8,128)(2,1)} %copy-done.65), kind=kOutput, calls=%fused_computation.52 | convolution fusion | flops 470670336 | bytes 23666688 | tf_op jit(solution)/shard_map/bqhe,bkhe->bhqk/dot_general | solution.py:63
  417.4 7.2 fusion.47
  441.7 8.9 %fusion.59 = bf16[3,384,2048]{2,1,0:T(8,128)(2,1)S(1)} fusion(bf16[3,384,2048]{2,1,0:T(8,128)(2,1)S(1)} %bitcast.560, bf16[3,384,512]{2,1,0:T(8,128)(2,1)S(1)} %fusion.319, bf16[2048,512]{1,0:T(8,128)(2,1)S(1)} %copy-done.147), kind=kOutput, calls=%fused_computation.125 | convolution fusion | flops 2470182912 | bytes 12713984 | tf_op jit(solution)/shard_map/bsd,fd->bsf/dot_general | solution.py:48
  464.6 7.7 %fusion.15 = (f32[3,8,384]{2,1,0:T(8,128)S(1)}, bf16[3,8,384,384]{2,3,1,0:T(8,128)(2,1)S(1)}) fusion(f32[3,8,384,384]{2,3,1,0:T(8,128)} %get-tuple-element.32, f32[3,8,384]{2,1,0:T(8,128)S(1)} %copy-done.83, bf16[3,384,8,64]{1,3,2,0:T(8,128)(2,1)S(1)} %convolution_convert_fusion.52, bf16[3,384,24,64]{1,3,2,0:T(8,128)(2,1)} %copy-done.61), kind=kOutput, calls=%fused_computation.57 | convolution fusion | flops 470670336 | bytes 23666688 | tf_op jit(solution)/shard_map/bqhe,bkhe->bhqk/dot_general | solution.py:63
  472.3 7.1 fusion.46
  496.6 8.7 %fusion.62 = bf16[3,384,2048]{2,1,0:T(8,128)(2,1)S(1)} fusion(bf16[3,384,2048]{2,1,0:T(8,128)(2,1)S(1)} %bitcast.556, bf16[3,384,512]{2,1,0:T(8,128)(2,1)S(1)} %fusion.317, bf16[2048,512]{1,0:T(8,128)(2,1)S(1)} %copy-done.148), kind=kOutput, calls=%fused_computation.128 | convolution fusion | flops 2470182912 | bytes 12713984 | tf_op jit(solution)/shard_map/bsd,fd->bsf/dot_general | solution.py:48
  519.7 8.1 %fusion.20 = (f32[3,8,384]{2,1,0:T(8,128)S(1)}, bf16[3,8,384,384]{2,3,1,0:T(8,128)(2,1)S(1)}) fusion(f32[3,8,384,384]{2,3,1,0:T(8,128)} %get-tuple-element.26, f32[3,8,384]{2,1,0:T(8,128)S(1)} %copy-done.81, bf16[3,384,8,64]{1,3,2,0:T(8,128)(2,1)S(1)} %convolution_convert_fusion.51, bf16[3,384,24,64]{1,3,2,0:T(8,128)(2,1)} %copy-done.55), kind=kOutput, calls=%fused_computation.62 | convolution fusion | flops 470670336 | bytes 23666688 | tf_op jit(solution)/shard_map/bqhe,bkhe->bhqk/dot_general | solution.py:63
  527.9 7.3 fusion.45
  549.2 12.7 %fusion.124 = f32[2048,512]{1,0:T(8,128)} fusion(f32[2048,512,1]{1,0,2:T(8,128)} %fusion.429, f32[2048,512,1]{1,0,2:T(8,128)} %fusion.426, f32[2048,512,1]{1,0,2:T(8,128)} %fusion.120, f32[2048,512,1]{1,0,2:T(8,128)} %fusion.435, f32[2048,512,1]{1,0,2:T(8,128)} %fusion.432, bf16[3,384,2048]{2,1,0:T(8,128)(2,1)} %copy-done.198, bf16[6,384,512]{2,1,0:T(8,128)(2,1)} %param.10), kind=kOutput, calls=%fused_computation.201 | convolution fusion | flops 2444754944 | bytes 31064064 | tf_op jit(solution)/shard_map/bsf,bsd->fd/dot_general | solution.py:47
  564.5 8.6 %fusion.125 = f32[512,2048]{1,0:T(8,128)} fusion(f32[512,2048,1]{1,0,2:T(8,128)S(1)} %copy-done.3, f32[512,2048,1]{1,0,2:T(8,128)S(1)} %copy-done.1, f32[512,2048,1]{1,0,2:T(8,128)} %fusion.361, f32[512,2048,1]{1,0,2:T(8,128)S(1)} %copy-done.4, f32[512,2048,1]{1,0,2:T(8,128)S(1)} %copy-done.2, bf16[3,384,2048]{2,1,0:T(8,128)(2,1)} %copy-done.17, ...), kind=kOutput, calls=%fused_computation.206 | convolution fusion | flops 2422931456 | bytes 31068672 | tf_op jit(solution)/shard_map/bsd,bsf->df/dot_general | solution.py:51
  573.2 11.0 %fusion.128 = f32[512,24,64]{0,2,1:T(8,128)} fusion(f32[512,24,64,1]{0,2,1,3:T(8,128)} %fusion.239, f32[512,24,64,1]{0,2,1,3:T(8,128)} %fusion.240, f32[512,24,64,1]{0,2,1,3:T(8,128)} %fusion.241, f32[512,24,64,1]{0,2,1,3:T(8,128)} %fusion.242, f32[512,24,64,1]{0,2,1,3:T(8,128)} %fusion.243, bf16[3,384,8,64]{1,3,2,0:T(8,128)(2,1)} %fusion.267, ...), kind=kOutput, calls=%fused_computation.283 | convolution fusion | flops 1830027264 | bytes 23600128 | tf_op jit(solution)/shard_map/bsd,bshe->dhe/dot_general | solution.py:69
  595.7 151.9 %all-reduce.3.cloned.1.call-done = (f32[512,24,64]{0,2,1:T(8,128)}, f32[8,64,512]{2,1,0:T(8,128)}, f32[512,2048]{1,0:T(8,128)}, f32[2048,512]{1,0:T(8,128)}) async-done(((f32[512,24,64]{0,2,1:T(8,128)}, f32[8,64,512]{2,1,0:T(8,128)}, f32[512,2048]{1,0:T(8,128)}, f32[2048,512]{1,0:T(8,128)}), (f32[512,24,64]{0,2,1:T(8,128)}, f32[8,64,512]{2,1,0:T(8,128)}, f32[512,2048]{1,0:T(8,128)}, ...) | async-done | bytes 12582928 | tf_op jit(solution)/shard_map/psum | solution.py:103
  (611 shorter events, 335.7 us)
Async XLA Ops:
  7.2 36.5 %copy-start = (bf16[512,2048]{1,0:T(8,128)(2,1)S(1)}, bf16[512,2048]{1,0:T(8,128)(2,1)}, u32[]{:S(2)}) copy-start(bf16[512,2048]{1,0:T(8,128)(2,1)} %param.16) | copy-start | bytes 6291460
  7.2 740.5 %all-reduce.3.cloned.1.call-start = ((), (), s32[]{:S(2)}) async-start(), calls=%async_computation | async-start | bytes 25165824 | tf_op jit(solution)/shard_map/psum | solution.py:103
  8.1 38.6 %copy-start.137 = (bf16[512]{0:T(512)(128)(2,1)}, bf16[512]{0:T(512)(128)(2,1)S(1)}, u32[]{:S(2)}) copy-start(bf16[512]{0:T(512)(128)(2,1)S(1)} %get-tuple-element.13) | copy-start | bytes 3076
  8.1 76.9 %copy-start.135 = (bf16[512]{0:T(512)(128)(2,1)}, bf16[512]{0:T(512)(128)(2,1)S(1)}, u32[]{:S(2)}) copy-start(bf16[512]{0:T(512)(128)(2,1)S(1)} %get-tuple-element.11) | copy-start | bytes 3076
  8.1 167.5 %copy-start.132 = (bf16[512]{0:T(512)(128)(2,1)}, bf16[512]{0:T(512)(128)(2,1)S(1)}, u32[]{:S(2)}) copy-start(bf16[512]{0:T(512)(128)(2,1)S(1)} %get-tuple-element.12) | copy-start | bytes 3076
  27.4 10.3 %copy-start.71 = (f32[3,8,384]{2,1,0:T(8,128)}, f32[3,8,384]{2,1,0:T(8,128)S(1)}, u32[]{:S(2)}) copy-start(f32[3,8,384]{2,1,0:T(8,128)S(1)} %get-tuple-element.43) | copy-start | bytes 110596
  50.9 29.6 %copy-start.43 = (bf16[3,384,512]{2,1,0:T(8,128)(2,1)}, bf16[3,384,512]{2,1,0:T(8,128)(2,1)S(1)}, u32[]{:S(2)}) copy-start(bf16[3,384,512]{2,1,0:T(8,128)(2,1)S(1)} %get-tuple-element.48) | copy-start | bytes 3538948
  65.4 10.3 %copy-start.75 = (f32[3,8,384]{2,1,0:T(8,128)}, f32[3,8,384]{2,1,0:T(8,128)S(1)}, u32[]{:S(2)}) copy-start(f32[3,8,384]{2,1,0:T(8,128)S(1)} %get-tuple-element.49) | copy-start | bytes 110596
  89.2 29.5 %copy-start.47 = (bf16[3,384,512]{2,1,0:T(8,128)(2,1)}, bf16[3,384,512]{2,1,0:T(8,128)(2,1)S(1)}, u32[]{:S(2)}) copy-start(bf16[3,384,512]{2,1,0:T(8,128)(2,1)S(1)} %get-tuple-element.54) | copy-start | bytes 3538948
  103.8 10.2 %copy-start.79 = (f32[3,8,384]{2,1,0:T(8,128)}, f32[3,8,384]{2,1,0:T(8,128)S(1)}, u32[]{:S(2)}) copy-start(f32[3,8,384]{2,1,0:T(8,128)S(1)} %get-tuple-element.55) | copy-start | bytes 110596
  119.8 22.3 %copy-start.28 = (bf16[3,384,512]{2,1,0:T(8,128)(2,1)}, bf16[3,384,512]{2,1,0:T(8,128)(2,1)S(1)}, u32[]{:S(2)}) copy-start(bf16[3,384,512]{2,1,0:T(8,128)(2,1)S(1)} %get-tuple-element.58) | copy-start | bytes 3538948
  119.8 22.3 %copy-start.87 = (f32[3,384]{1,0:T(4,128)}, f32[3,384]{1,0:T(4,128)S(1)}, u32[]{:S(2)}) copy-start(f32[3,384]{1,0:T(4,128)S(1)} %fusion.399) | copy-start | bytes 13828
  160.6 10.2 %copy-start.69 = (f32[3,8,384]{2,1,0:T(8,128)}, f32[3,8,384]{2,1,0:T(8,128)S(1)}, u32[]{:S(2)}) copy-start(f32[3,8,384]{2,1,0:T(8,128)S(1)} %get-tuple-element.25) | copy-start | bytes 110596
  184.0 29.8 %copy-start.41 = (bf16[3,384,512]{2,1,0:T(8,128)(2,1)}, bf16[3,384,512]{2,1,0:T(8,128)(2,1)S(1)}, u32[]{:S(2)}) copy-start(bf16[3,384,512]{2,1,0:T(8,128)(2,1)S(1)} %get-tuple-element.30) | copy-start | bytes 3538948
  198.8 10.2 %copy-start.73 = (f32[3,8,384]{2,1,0:T(8,128)}, f32[3,8,384]{2,1,0:T(8,128)S(1)}, u32[]{:S(2)}) copy-start(f32[3,8,384]{2,1,0:T(8,128)S(1)} %get-tuple-element.31) | copy-start | bytes 110596
  222.7 29.6 %copy-start.45 = (bf16[3,384,512]{2,1,0:T(8,128)(2,1)}, bf16[3,384,512]{2,1,0:T(8,128)(2,1)S(1)}, u32[]{:S(2)}) copy-start(bf16[3,384,512]{2,1,0:T(8,128)(2,1)S(1)} %get-tuple-element.36) | copy-start | bytes 3538948
  237.2 10.2 %copy-start.77 = (f32[3,8,384]{2,1,0:T(8,128)}, f32[3,8,384]{2,1,0:T(8,128)S(1)}, u32[]{:S(2)}) copy-start(f32[3,8,384]{2,1,0:T(8,128)S(1)} %get-tuple-element.37) | copy-start | bytes 110596
  256.3 8.5 %copy-start.198 = (bf16[3,384,2048]{2,1,0:T(8,128)(2,1)}, bf16[3,384,2048]{2,1,0:T(8,128)(2,1)S(1)}, u32[]{:S(2)}) copy-start(bf16[3,384,2048]{2,1,0:T(8,128)(2,1)S(1)} %convolution_convert_fusion.15) | copy-start | bytes 14155780
  274.8 29.2 %copy-start.7 = (bf16[3,384,512]{2,1,0:T(8,128)(2,1)}, bf16[3,384,512]{2,1,0:T(8,128)(2,1)S(1)}, u32[]{:S(2)}) copy-start(bf16[3,384,512]{2,1,0:T(8,128)(2,1)S(1)} %get-tuple-element.24) | copy-start | bytes 3538948
  310.9 8.6 %copy-start.25 = (bf16[3,384,512]{2,1,0:T(8,128)(2,1)S(1)}, bf16[3,384,512]{2,1,0:T(8,128)(2,1)}, u32[]{:S(2)}) copy-start(bf16[3,384,512]{2,1,0:T(8,128)(2,1)} %copy-done.24) | copy-start | bytes 3538948
  365.6 8.9 %copy-start.15 = (bf16[3,384,512]{2,1,0:T(8,128)(2,1)S(1)}, bf16[3,384,512]{2,1,0:T(8,128)(2,1)}, u32[]{:S(2)}) copy-start(bf16[3,384,512]{2,1,0:T(8,128)(2,1)} %copy-done.14) | copy-start | bytes 3538948
  441.7 8.9 %copy-start.23 = (bf16[3,384,512]{2,1,0:T(8,128)(2,1)S(1)}, bf16[3,384,512]{2,1,0:T(8,128)(2,1)}, u32[]{:S(2)}) copy-start(bf16[3,384,512]{2,1,0:T(8,128)(2,1)} %copy-done.22) | copy-start | bytes 3538948
  496.6 8.7 %copy-start.19 = (bf16[3,384,512]{2,1,0:T(8,128)(2,1)S(1)}, bf16[3,384,512]{2,1,0:T(8,128)(2,1)}, u32[]{:S(2)}) copy-start(bf16[3,384,512]{2,1,0:T(8,128)(2,1)} %copy-done.18) | copy-start | bytes 3538948
  519.7 25.4 %copy-start.35 = (bf16[3,384,8,64]{1,3,2,0:T(8,128)(2,1)}, bf16[3,384,8,64]{1,3,2,0:T(8,128)(2,1)S(1)}, u32[]{:S(2)}) copy-start(bf16[3,384,8,64]{1,3,2,0:T(8,128)(2,1)S(1)} %fusion.264) | copy-start | bytes 3538948
  519.7 8.1 %copy-start.70 = (f32[3,8,384]{2,1,0:T(8,128)S(1)}, f32[3,8,384]{2,1,0:T(8,128)}, u32[]{:S(2)}) copy-start(f32[3,8,384]{2,1,0:T(8,128)} %copy-done.69) | copy-start | bytes 110596
  549.2 12.8 %copy-start.1 = (f32[512,2048,1]{1,0,2:T(8,128)S(1)}, f32[512,2048,1]{1,0,2:T(8,128)}, u32[]{:S(2)}) copy-start(f32[512,2048,1]{1,0,2:T(8,128)} %fusion.347) | copy-start | bytes 12582916
  549.2 12.8 %copy-start.2 = (f32[512,2048,1]{1,0,2:T(8,128)S(1)}, f32[512,2048,1]{1,0,2:T(8,128)}, u32[]{:S(2)}) copy-start(f32[512,2048,1]{1,0,2:T(8,128)} %fusion.355) | copy-start | bytes 12582916
  549.2 13.9 %copy-start.3 = (f32[512,2048,1]{1,0,2:T(8,128)S(1)}, f32[512,2048,1]{1,0,2:T(8,128)}, u32[]{:S(2)}) copy-start(f32[512,2048,1]{1,0,2:T(8,128)} %fusion.350) | copy-start | bytes 12582916
  549.2 15.1 %copy-start.4 = (f32[512,2048,1]{1,0,2:T(8,128)S(1)}, f32[512,2048,1]{1,0,2:T(8,128)}, u32[]{:S(2)}) copy-start(f32[512,2048,1]{1,0,2:T(8,128)} %fusion.358) | copy-start | bytes 12582916
  549.2 15.3 %copy-start.16 = (bf16[3,384,512]{2,1,0:T(8,128)(2,1)S(1)}, bf16[3,384,512]{2,1,0:T(8,128)(2,1)}, u32[]{:S(2)}) copy-start(bf16[3,384,512]{2,1,0:T(8,128)(2,1)} %copy-done.14) | copy-start | bytes 3538948
  549.2 15.3 %copy-start.101 = (f32[3,384]{1,0:T(4,128)S(1)}, f32[3,384]{1,0:T(4,128)}, u32[]{:S(2)}) copy-start(f32[3,384]{1,0:T(4,128)} %copy-done.99) | copy-start | bytes 13828
  564.5 8.6 %copy-start.103 = (f32[3,384]{1,0:T(4,128)S(1)}, f32[3,384]{1,0:T(4,128)}, u32[]{:S(2)}) copy-start(f32[3,384]{1,0:T(4,128)} %copy-done.102) | copy-start | bytes 13828
  (196 other events, 690.8 us)
Sparse Core Ops, SparseCore 0:
  584.3 163.2 all-reduce.2
where the time goes:
time: 770 us; the launch traced here: 765 us
  matrix products  394 us (51%)
  other arithmetic  161 us (21%)
  waiting for transfers between devices  152 us (20%)
  local copies, waits for them, and re-layouts  40.8 us (5%)
  between operations  17.2 us (2%)
    psum x1, waiting for transfers between devices, per_device(): reduced = lax.psum(micro_grads, 'data')  152 us
    convert_element_type x6, other arithmetic, attn_probs(): jax.nn.softmax(scores.astype(jnp.float32) * attn_scale, axis=-1)  57.6 us
    dot_general x6, matrix products, layer_bwd(): jnp.einsum('bsd,fd->bsf', d_out, w_down, preferred_element_type=jnp.float32)  52.4 us
    dot_general x6, matrix products, layer_bwd(): jnp.einsum('bqhe,bkhe->bhqk', d_mix, v_heads, preferred_element_type=jnp....  46.5 us
    convert_element_type x6, other arithmetic, attn_probs(): scores.astype(jnp.float32) * attn_scale  43.2 us
    dot_general x6, matrix products, layer_bwd(): jnp.einsum('bsf,bsd->fd', g_act, d_out, preferred_element_type=jnp.float32)  42.3 us
    sub x6, other arithmetic, attn_probs(): jax.nn.softmax(scores.astype(jnp.float32) * attn_scale, axis=-1)  42 us
    unnamed x457, local copies, waits for them, and re-layouts  36.2 us
  transfers between devices with their start and end apart: 1, of which 1 were waited for; matrix products, arithmetic and copies ran while one was open for 1% of the time, Pallas kernels for 0%

commit v1 on v0

v1 whole, which is shorter than its diff:
```python
import functools

import jax
import jax.numpy as jnp
from jax import lax
from jax.experimental import pallas as pl
from jax.experimental.pallas import tpu as pltpu
from jax.sharding import PartitionSpec as P

NORM_EPS = 1e-6
BF = jnp.bfloat16
F32 = jnp.float32
GELU_C = 0.7978845608028654
GELU_A = 0.044715


def mm(a, b):
    return lax.dot_general(a, b, (((1,), (0,)), ((), ())), preferred_element_type=F32)


def mm_nt(a, b):
    return lax.dot_general(a, b, (((1,), (1,)), ((), ())), preferred_element_type=F32)


def mm_tn(a, b):
    return lax.dot_general(a, b, (((0,), (0,)), ((), ())), preferred_element_type=F32)


def rms_scale(xf):
    return lax.rsqrt(jnp.mean(xf * xf, axis=-1, keepdims=True) + NORM_EPS)


def rms_bwd(x, dy):
    xf = x.astype(F32)
    gf = dy.astype(F32)
    r = rms_scale(xf)
    dot = jnp.mean(xf * gf, axis=-1, keepdims=True)
    return (gf * r - xf * (r * r * r * dot)).astype(BF)


def gelu_fwd(z):
    zf = z.astype(F32)
    t = jnp.tanh(GELU_C * (zf + GELU_A * (zf * zf * zf)))
    return (zf * (0.5 * (1.0 + t))).astype(BF)


def gelu_bwd(z, dg):
    zf = z.astype(F32)
    z2 = zf * zf
    t = jnp.tanh(GELU_C * (zf + GELU_A * (zf * z2)))
    slope = 0.5 * (1.0 + t) + (0.5 * zf) * (1.0 - t * t) * (GELU_C + (3.0 * GELU_C * GELU_A) * z2)
    return (dg.astype(F32) * slope).astype(BF)


def head_stack(a4, n_sub, width):
    lane = lax.broadcasted_iota(jnp.int32, a4.shape, 1)
    zero = jnp.zeros_like(a4)
    return jnp.concatenate([jnp.where((lane >= h * width) & (lane < (h + 1) * width), a4, zero) for h in range(n_sub)], axis=0)


def step_kernel(cfg, x_ref, g_ref, emb_ref, wqkv_ref, wo_ref, wup_ref, wdn_ref,
                dx_ref, gqkv_ref, go_ref, gup_ref, gdn_ref,
                xs, uT, qkv, st, stat, mixT, hs, mT, zs, gs, dmid, doutT, dcur,
                a_qkv, a_o, a_up, a_dn, sem):
    S, D, FF, HW, L = cfg
    QW = 256
    NQ = D // QW
    NS = QW // HW
    scale = HW ** -0.5
    step = pl.program_id(0)
    last = pl.num_programs(0) - 1

    @pl.when(step == 0)
    def _():
        a_qkv[...] = jnp.zeros_like(a_qkv)
        a_o[...] = jnp.zeros_like(a_o)
        a_up[...] = jnp.zeros_like(a_up)
        a_dn[...] = jnp.zeros_like(a_dn)

    xs[0] = x_ref[0] + emb_ref[0].astype(BF)

    def fwd(l, carry):
        rows = pl.ds(pl.multiple_of(l * S, S), S)
        x = xs[l]
        xf = x.astype(F32)
        u = (xf * rms_scale(xf)).astype(BF)
        uT[:, rows] = u.T
        for j in range(3):
            cols = slice(j * D, (j + 1) * D)
            qkv[rows, cols] = mm(u, wqkv_ref[:, cols]).astype(BF)
        for c in range(NQ):
            q4 = qkv[rows, c * QW:(c + 1) * QW]
            k4 = qkv[rows, D + c * QW:D + (c + 1) * QW]
            v4 = qkv[rows, 2 * D + c * QW:2 * D + (c + 1) * QW]
            qm = head_stack(q4, NS, HW)
            vT = v4.T
            for pr in range(NS // 2):
                cols = slice(pr * 2 * S, (pr + 1) * 2 * S)
                sb = mm_nt(k4, qm[cols]).astype(BF)
                st[l, c, :, cols] = sb
                s = sb.astype(F32)
                m = jnp.max(s, axis=0, keepdims=True)
                e = jnp.exp((s - m) * scale)
                inv = 1.0 / jnp.sum(e, axis=0, keepdims=True)
                stat[l, c, 0:1, cols] = m
                stat[l, c, 1:2, cols] = inv
                p = (e * inv).astype(BF)
                for hh in range(2):
                    h = pr * 2 + hh
                    o = mm(vT[h * HW:(h + 1) * HW], p[:, hh * S:(hh + 1) * S])
                    mixT[c * QW + h * HW:c * QW + (h + 1) * HW, rows] = o.astype(BF)
        h_mid = x + mm_tn(mixT[:, rows], wo_ref[...]).astype(BF)
        hs[l] = h_mid
        hf = h_mid.astype(F32)
        mn = (hf * rms_scale(hf)).astype(BF)
        mT[:, rows] = mn.T
        for j in range(FF // D):
            cols = slice(j * D, (j + 1) * D)
            z = mm(mn, wup_ref[:, cols]).astype(BF)
            zs[rows, cols] = z
            gs[rows, cols] = gelu_fwd(z)

        @pl.when(l < L - 1)
        def _():
            y = mm(gs[rows, :], wdn_ref[...]).astype(BF)
            xs[l + 1] = (h_mid + y) + emb_ref[l + 1].astype(BF)
        return carry

    lax.fori_loop(0, L, fwd, 0)
    dcur[...] = g_ref[0]

    def bwd(i, carry):
        l = L - 1 - i
        rows = pl.ds(pl.multiple_of(l * S, S), S)
        d_out = dcur[...]
        doutT[:, rows] = d_out.T
        for j in range(FF // D):
            cols = slice(j * D, (j + 1) * D)
            d_act = mm_nt(d_out, wdn_ref[cols, :]).astype(BF)
            zs[rows, cols] = gelu_bwd(zs[rows, cols], d_act)
        d_norm = mm_nt(zs[rows, :], wup_ref[...]).astype(BF)
        d_mid = d_out + rms_bwd(hs[l], d_norm)
        dmid[rows, :] = d_mid
        d_mix = mm_nt(d_mid, wo_ref[...]).astype(BF)
        for c in range(NQ):
            qc = slice(c * QW, (c + 1) * QW)
            kc = slice(D + c * QW, D + (c + 1) * QW)
            vc = slice(2 * D + c * QW, 2 * D + (c + 1) * QW)
            q4 = qkv[rows, qc]
            k4 = qkv[rows, kc]
            v4 = qkv[rows, vc]
            qm = head_stack(q4, NS, HW)
            dom = head_stack(d_mix[:, qc], NS, HW)
            kT = k4.T
            dv = None
            dk = None
            dqT = []
            for pr in range(NS // 2):
                cols = slice(pr * 2 * S, (pr + 1) * 2 * S)
                dp = mm_nt(v4, dom[cols]).astype(BF).astype(F32)
                s = st[l, c, :, cols].astype(F32)
                p = jnp.exp((s - stat[l, c, 0:1, cols]) * scale) * stat[l, c, 1:2, cols]
                dv_p = mm(p.astype(BF), dom[cols])
                delta = jnp.sum(dp * p, axis=0, keepdims=True)
                ds = ((p * (dp - delta)) * scale).astype(BF)
                dk_p = mm(ds, qm[cols])
                dv = dv_p if dv is None else dv + dv_p
                dk = dk_p if dk is None else dk + dk_p
                for hh in range(2):
                    h = pr * 2 + hh
                    dqT.append(mm(kT[h * HW:(h + 1) * HW], ds[:, hh * S:(hh + 1) * S]).astype(BF))
            qkv[rows, qc] = jnp.concatenate(dqT, axis=0).T
            qkv[rows, kc] = dk.astype(BF)
            qkv[rows, vc] = dv.astype(BF)
        d_norm_x = mm_nt(qkv[rows, :], wqkv_ref[...]).astype(BF)
        dcur[...] = d_mid + rms_bwd(xs[l], d_norm_x)
        return carry

    lax.fori_loop(0, L, bwd, 0)
    dx_ref[0] = dcur[...]

    def wg(acc, lhs, rhs, n):
        def body(j, carry):
            cols = pl.ds(pl.multiple_of(j * D, D), D)
            acc[:, cols] = acc[:, cols] + mm(lhs[...], rhs[:, cols])
            return carry
        lax.fori_loop(0, n, body, 0)

    wg(a_qkv, uT, qkv, 3)
    wg(a_o, mixT, dmid, 1)
    wg(a_up, mT, zs, FF // D)
    wg(a_dn, doutT, gs, FF // D)

    @pl.when(step == last)
    def _():
        pairs = ((a_qkv, gqkv_ref), (a_o, go_ref), (a_up, gup_ref), (a_dn, gdn_ref))
        copies = [pltpu.make_async_copy(s_, d_, sem.at[i]) for i, (s_, d_) in enumerate(pairs)]
        for cp in copies:
            cp.start()
        for cp in copies:
            cp.wait()


def local_grads(x, g, emb, wqkv, wo, wup, wdn, HW):
    B, S, D = x.shape
    FF = wup.shape[1]
    L = emb.shape[0]
    emb = emb.astype(F32).reshape(L, 1, D)
    T = L * S
    NQ = D // 256
    NS = 256 // HW
    const = lambda shape: pl.BlockSpec(shape, lambda b: (0,) * len(shape), pipeline_mode=pl.Buffered(1))
    seq = pl.BlockSpec((1, S, D), lambda b: (b, 0, 0))
    hbm = pl.BlockSpec(memory_space=pl.ANY)
    return pl.pallas_call(
        functools.partial(step_kernel, (S, D, FF, HW, L)),
        name='block_grads',
        grid=(B,),
        in_specs=[seq, seq, const(emb.shape), const(wqkv.shape), const(wo.shape), const(wup.shape), const(wdn.shape)],
        out_specs=[seq, hbm, hbm, hbm, hbm],
        out_shape=[
            jax.ShapeDtypeStruct(x.shape, BF),
            jax.ShapeDtypeStruct((D, 3 * D), F32),
            jax.ShapeDtypeStruct((D, D), F32),
            jax.ShapeDtypeStruct((D, FF), F32),
            jax.ShapeDtypeStruct((D, FF), F32),
        ],
        scratch_shapes=[
            pltpu.VMEM((L, S, D), BF),
            pltpu.VMEM((D, T), BF),
            pltpu.VMEM((T, 3 * D), BF),
            pltpu.VMEM((L, NQ, S, NS * S), BF),
            pltpu.VMEM((L, NQ, 8, NS * S), F32),
            pltpu.VMEM((D, T), BF),
            pltpu.VMEM((L, S, D), BF),
            pltpu.VMEM((D, T), BF),
            pltpu.VMEM((T, FF), BF),
            pltpu.VMEM((T, FF), BF),
            pltpu.VMEM((T, D), BF),
            pltpu.VMEM((D, T), BF),
            pltpu.VMEM((S, D), BF),
            pltpu.VMEM((D, 3 * D), F32),
            pltpu.VMEM((D, D), F32),
            pltpu.VMEM((D, FF), F32),
            pltpu.VMEM((D, FF), F32),
            pltpu.SemaphoreType.DMA((4,)),
        ],
        compiler_params=pltpu.CompilerParams(dimension_semantics=('arbitrary',), vmem_limit_bytes=67043328),
    )(x, g, emb, wqkv, wo, wup, wdn)


def solution(mesh):
    batch_spec = P('data', None, None)

    def per_device(x_loc, g_loc, step_emb, w_q, w_k, w_v, w_o, w_up, w_down):
        D, H, HW = w_q.shape
        wqkv = jnp.concatenate([w.reshape(D, H * HW) for w in (w_q, w_k, w_v)], axis=1)
        d_x, gqkv, go, gup, gdnT = local_grads(x_loc, g_loc, step_emb, wqkv, w_o.reshape(H * HW, D), w_up, w_down, HW)
        gqkv, go, gup, gdnT = lax.psum((gqkv, go, gup, gdnT), 'data')
        parts = [gqkv[:, i * H * HW:(i + 1) * H * HW].reshape(D, H, HW) for i in range(3)]
        return (parts[0], parts[1], parts[2], go.reshape(H, HW, D), gup, gdnT.T, d_x)

    return jax.shard_map(per_device, mesh=mesh, in_specs=(batch_spec, batch_spec, P(), P(), P(), P(), P(), P(), P()), out_specs=(P(), P(), P(), P(), P(), P(), batch_spec), check_vma=False)
```

time: 770 us -> 535 us (0.69)
  matrix products: 394 us -> 0 us
  Pallas kernels: 0 us -> 334 us
  other arithmetic: 161 us -> 1.26 us
  local copies, waits for them, and re-layouts: 40.8 us -> 22.2 us
  waiting for transfers between devices: 152 us -> 163 us
    dot_general x106 -> x0, matrix products: 394 us -> none  [the longest x6 52.4 us: layer_bwd(): jnp.einsum('bsd,fd->bsf', d_out, w_down, preferred_element_type=jnp.float32)]
    pallas_call x0 -> x1, Pallas kernels: none -> 334 us  [local_grads(): pl.pallas_call(functools.partial(step_kernel, (S, D, FF, HW, L)), name='b...]
    convert_element_type x12 -> x0, other arithmetic: 101 us -> none  [the longest x6 57.6 us: attn_probs(): jax.nn.softmax(scores.astype(jnp.float32) * attn_scale, axis=-1)]
    sub x6 -> x0, other arithmetic: 42 us -> none  [attn_probs(): jax.nn.softmax(scores.astype(jnp.float32) * attn_scale, axis=-1)]
    unnamed x457 -> x5, local copies, waits for them, and re-layouts: 36.2 us -> 11.1 us
    psum x1, waiting for transfers between devices: 152 us -> 163 us  [per_device(): gqkv, go, gup, gdnT = lax.psum((gqkv, go, gup, gdnT), 'data')]
    add x10 -> x0, other arithmetic: 9.83 us -> none  [the longest x5 5.26 us: layer_bwd(): d_mid = d_out + d_mid_norm]
  transfers between devices with their start and end apart: 1 -> 1, of which waited for: 1 -> 1; matrix products, arithmetic and copies ran while one was open for 1% -> 0% of each run, Pallas kernels for 0% -> 0%
where the time goes in v1:
time: 535 us
  Pallas kernels  334 us (62%)
  waiting for transfers between devices  163 us (30%)
  local copies, waits for them, and re-layouts  22.2 us (4%)
  between operations  14.1 us (3%)
    pallas_call x1, Pallas kernels, local_grads(): pl.pallas_call(functools.partial(step_kernel, (S, D, FF, HW, L)), name='b...  334 us
    psum x1, waiting for transfers between devices, per_device(): gqkv, go, gup, gdnT = lax.psum((gqkv, go, gup, gdnT), 'data')  163 us
    unnamed x5, local copies, waits for them, and re-layouts  11.1 us
  transfers between devices with their start and end apart: 1, of which 1 were waited for; matrix products, arithmetic and copies ran while one was open for 0% of the time, Pallas kernels for 0%

profile of v1, /device:TPU:0, one launch (start us, length us, event | category | flops | bytes accessed | tf_op | source)
XLA Modules:
  0.0 534.6 jit_solution(16398606732815902217)
XLA Ops:
  7.2 0.0 all-reduce.3.cloned.1.call-start
  7.2 1.3 reshape.54.emb_ref
  8.5 1.3 copy.23
  9.8 1.3 copy.24
  11.0 1.3 copy.25
  12.3 1.3 pad_maximum_fusion.wqkv_ref
  13.5 333.6 %block_grads.1 = (bf16[6,384,512]{2,1,0:T(8,128)(2,1)}, f32[512,1536]{1,0:T(8,128)}, f32[512,512]{1,0:T(8,128)}, f32[512,2048]{1,0:T(8,128)}, f32[512,2048]{1,0:T(8,128)}) custom-call(bf16[6,384,512]{2,1,0:T(8,128)(2,1)} %x_ref.1, bf16[6,384,512]{2,1,0:T(8,128)(2,1)} %g_ref.1, f32[3,1,512]{2,1,0:T(1,128)} %reshape.54.emb_ref, ...), custom_call_target="tpu_custom_call" | custom-call | tf_op jit(solution)/shard_map/block_grads/pallas_call | solution.py:215
  347.1 0.0 all-reduce.3.cloned.1.call-update
  347.1 163.5 %all-reduce.3.cloned.1.call-done = (f32[512,1536]{1,0:T(8,128)}, f32[8,64,512]{2,1,0:T(8,128)}, f32[512,2048]{1,0:T(8,128)}, f32[2048,512]{0,1:T(8,128)}) async-done(((f32[512,1536]{1,0:T(8,128)}, f32[8,64,512]{2,1,0:T(8,128)}, f32[512,2048]{1,0:T(8,128)}, f32[2048,512]{0,1:T(8,128)}), (f32[512,1536]{1,0:T(8,128)}, f32[8,64,512]{2,1,0:T(8,128)}, f32[512,2048]{1,0:T(8,128)}, ...) | async-done | bytes 12582928 | tf_op jit(solution)/shard_map/psum | solution.py:259
  510.6 2.2 fusion
  512.8 1.3 copy.28
  514.1 1.3 copy.27
  515.4 1.3 copy.26
  516.7 0.0 copy-start
  516.7 5.4 %copy.29 = f32[2048,512]{1,0:T(8,128)} copy(f32[2048,512]{0,1:T(8,128)} %get-tuple-element.34) | data formatting | bytes 8388608
  522.1 0.0 copy-done
  522.1 1.0 copy.34
  523.1 4.7 copy.35
Async XLA Ops:
  7.2 503.4 %all-reduce.3.cloned.1.call-start = ((), (), s32[]{:S(2)}) async-start(), calls=%async_computation | async-start | bytes 25165824 | tf_op jit(solution)/shard_map/psum | solution.py:259
  516.7 5.4 %copy-start = (f32[8,64,512]{2,1,0:T(8,128)S(1)}, f32[8,64,512]{2,1,0:T(8,128)}, u32[]{:S(2)}) copy-start(f32[8,64,512]{2,1,0:T(8,128)} %get-tuple-element.41) | copy-start | bytes 3145732
Sparse Core Ops, SparseCore 0:
  347.2 163.2 all-reduce.2

commit v2 on v1

v2 whole, which is shorter than its diff:
```python
import functools

import jax
import jax.numpy as jnp
from jax import lax
from jax.experimental import pallas as pl
from jax.experimental.pallas import tpu as pltpu
from jax.sharding import PartitionSpec as P

NORM_EPS = 1e-6
BF = jnp.bfloat16
F32 = jnp.float32
GELU_C = 0.7978845608028654
GELU_A = 0.044715
LOG2E = 1.4426950408889634
MESH = pl.DeviceIdType.MESH
UNIT = 512
QW = 256
VMEM_MAX = 67043328


def mm(a, b):
    return lax.dot_general(a, b, (((1,), (0,)), ((), ())), preferred_element_type=F32)


def mm_nt(a, b):
    return lax.dot_general(a, b, (((1,), (1,)), ((), ())), preferred_element_type=F32)


def mm_tn(a, b):
    return lax.dot_general(a, b, (((0,), (0,)), ((), ())), preferred_element_type=F32)


def rms_scale(xf):
    return lax.rsqrt(jnp.mean(xf * xf, axis=-1, keepdims=True) + NORM_EPS)


def rms_bwd(x, dy):
    xf = x.astype(F32)
    gf = dy.astype(F32)
    r = rms_scale(xf)
    dot = jnp.mean(xf * gf, axis=-1, keepdims=True)
    return (gf * r - xf * (r * r * r * dot)).astype(BF)


def gelu_fwd(z):
    zf = z.astype(F32)
    t = jnp.tanh(zf * (GELU_C + (GELU_C * GELU_A) * (zf * zf)))
    half = 0.5 * zf
    return (half + half * t).astype(BF)


def gelu_bwd(z, dg):
    zf = z.astype(F32)
    z2 = zf * zf
    t = jnp.tanh(zf * (GELU_C + (GELU_C * GELU_A) * z2))
    slope = (0.5 + 0.5 * t) + (1.0 - t * t) * (zf * ((0.5 * GELU_C) + (1.5 * GELU_C * GELU_A) * z2))
    return (dg.astype(F32) * slope).astype(BF)


def head_stack(a4, width):
    lane = lax.broadcasted_iota(jnp.int32, a4.shape, 1)
    zero = jnp.zeros_like(a4)
    n_sub = a4.shape[1] // width
    return jnp.concatenate([jnp.where((lane >= h * width) & (lane < (h + 1) * width), a4, zero) for h in range(n_sub)], axis=0)


def soft_stats(sb, scale):
    m = jnp.max(sb, axis=0, keepdims=True).astype(F32)
    e = jnp.exp2((sb.astype(F32) - m) * (scale * LOG2E))
    inv = 1.0 / jnp.sum(e, axis=0, keepdims=True)
    return m, e, inv


def attn_bwd_quad(q4, k4, v4, do4, HW, get_p):
    S = q4.shape[0]
    ns = QW // HW
    scale = HW ** -0.5
    qm = head_stack(q4, HW)
    dom = head_stack(do4, HW)
    kT = k4.T
    dv = None
    dk = None
    dqT = []
    for pr in range(ns // 2):
        cols = slice(pr * 2 * S, (pr + 1) * 2 * S)
        p = get_p(qm[cols], k4, cols)
        dp = mm_nt(v4, dom[cols]).astype(BF).astype(F32)
        dv_p = mm(p.astype(BF), dom[cols])
        delta = jnp.sum(dp * p, axis=0, keepdims=True)
        ds = ((p * (dp - delta)) * scale).astype(BF)
        dk_p = mm(ds, qm[cols])
        dv = dv_p if dv is None else dv + dv_p
        dk = dk_p if dk is None else dk + dk_p
        for hh in range(2):
            h = pr * 2 + hh
            dqT.append(mm(kT[h * HW:(h + 1) * HW], ds[:, hh * S:(hh + 1) * S]).astype(BF))
    return jnp.concatenate(dqT, axis=0).T, dk.astype(BF), dv.astype(BF)


def step_kernel(cfg, x_ref, g_ref, emb_ref, wq_h, wk_h, wv_h, wo_ref, wup_ref, wdn_ref,
                acc_h, qkv0_ref, u0_ref, mix0_ref, dmid0_ref,
                xs, us, qkv, st, stat, mixT, hs, mT, zs, gs, dmid, dout, dcur, wqkvT, acc, sem, wsem):
    S, D, FF, HW, L = cfg
    NQ = D // QW
    NS = QW // HW
    scale = HW ** -0.5
    step = pl.program_id(0)
    last = pl.num_programs(0) - 1
    n_ff = FF // UNIT

    @pl.when(step == 0)
    def _():
        loads = [pltpu.make_async_copy(w, wqkvT.at[j * D:(j + 1) * D], wsem.at[j]) for j, w in enumerate((wq_h, wk_h, wv_h))]
        for cp in loads:
            cp.start()
        acc[...] = jnp.zeros_like(acc)
        for cp in loads:
            cp.wait()

    emb = emb_ref[...].astype(F32)
    xs[0] = x_ref[0] + emb[0:1].astype(BF)

    def fwd(l, carry):
        rows = pl.ds(pl.multiple_of(l * S, S), S)
        x = xs[l]
        xf = x.astype(F32)
        u = (xf * rms_scale(xf)).astype(BF)
        us[rows, :] = u
        for j in range(3):
            cols = slice(j * D, (j + 1) * D)
            qkv[rows, cols] = mm_nt(u, wqkvT[cols, :]).astype(BF)
        for c in range(NQ):
            q4 = qkv[rows, c * QW:(c + 1) * QW]
            k4 = qkv[rows, D + c * QW:D + (c + 1) * QW]
            v4 = qkv[rows, 2 * D + c * QW:2 * D + (c + 1) * QW]
            qm = head_stack(q4, HW)
            vT = v4.T
            for pr in range(NS // 2):
                cols = slice(pr * 2 * S, (pr + 1) * 2 * S)
                sb = mm_nt(k4, qm[cols]).astype(BF)
                st[l, c, :, cols] = sb
                m, e, inv = soft_stats(sb, scale)
                stat[l, c, 0:1, cols] = m
                stat[l, c, 1:2, cols] = inv
                p = (e * inv).astype(BF)
                for hh in range(2):
                    h = pr * 2 + hh
                    o = mm(vT[h * HW:(h + 1) * HW], p[:, hh * S:(hh + 1) * S])
                    mixT[c * QW + h * HW:c * QW + (h + 1) * HW, rows] = o.astype(BF)
        h_mid = x + mm_tn(mixT[:, rows], wo_ref[...]).astype(BF)
        hs[l] = h_mid
        hf = h_mid.astype(F32)
        mn = (hf * rms_scale(hf)).astype(BF)
        mT[:, rows] = mn.T
        for j in range(n_ff):
            cols = slice(j * UNIT, (j + 1) * UNIT)
            z = mm(mn, wup_ref[:, cols]).astype(BF)
            zs[rows, cols] = z
            gs[rows, cols] = gelu_fwd(z)

        @pl.when(l < L - 1)
        def _():
            y = mm(gs[rows, :], wdn_ref[...]).astype(BF)
            nxt = emb[1:2]
            for j in range(2, L):
                nxt = jnp.where(l + 1 == j, emb[j:j + 1], nxt)
            xs[l + 1] = (h_mid + y) + nxt.astype(BF)
        return carry

    lax.fori_loop(0, L, fwd, 0)
    dcur[...] = g_ref[0]
    qkv0_ref[0] = qkv[0:S, :]
    u0_ref[0] = us[0:S, :]
    mix0_ref[...] = mixT[:, 0:S]

    def bwd(i, carry):
        l = L - 1 - i
        rows = pl.ds(pl.multiple_of(l * S, S), S)
        d_out = dcur[...]
        dout[rows, :] = d_out
        for j in range(n_ff):
            cols = slice(j * UNIT, (j + 1) * UNIT)
            d_act = mm_nt(d_out, wdn_ref[cols, :]).astype(BF)
            zs[rows, cols] = gelu_bwd(zs[rows, cols], d_act)
        d_norm = mm_nt(zs[rows, :], wup_ref[...]).astype(BF)
        dmid[rows, :] = d_out + rms_bwd(hs[l], d_norm)

        @pl.when(l > 0)
        def _():
            d_mid = dmid[rows, :]
            d_mix = mm_nt(d_mid, wo_ref[...]).astype(BF)
            for c in range(NQ):
                qc = slice(c * QW, (c + 1) * QW)
                kc = slice(D + c * QW, D + (c + 1) * QW)
                vc = slice(2 * D + c * QW, 2 * D + (c + 1) * QW)

                def get_p(qs, k4, cols):
                    s = st[l, c, :, cols].astype(F32)
                    return jnp.exp2((s - stat[l, c, 0:1, cols]) * (scale * LOG2E)) * stat[l, c, 1:2, cols]

                dq, dk, dv = attn_bwd_quad(qkv[rows, qc], qkv[rows, kc], qkv[rows, vc], d_mix[:, qc], HW, get_p)
                qkv[rows, qc] = dq
                qkv[rows, kc] = dk
                qkv[rows, vc] = dv
            d_norm_x = mm(qkv[rows, :], wqkvT[...]).astype(BF)
            dcur[...] = d_mid + rms_bwd(xs[l], d_norm_x)
        return carry

    lax.fori_loop(0, L, bwd, 0)
    dmid0_ref[0] = dmid[0:S, :]

    def flush(k):
        @pl.when(step == last)
        def _():
            pltpu.make_async_copy(acc.at[k], acc_h.at[k], sem.at[k]).start()

    def attn_unit(j, carry):
        cols = pl.ds(pl.multiple_of(j * UNIT, UNIT), UNIT)
        acc[8 + j] = acc[8 + j] + mm_tn(qkv[S:, cols], us[S:, :])
        flush(8 + j)
        return carry

    lax.fori_loop(0, 3, attn_unit, 0)
    acc[11] = acc[11] + mm(mixT[:, S:], dmid[S:, :])
    flush(11)

    def mlp_unit(j, carry):
        cols = pl.ds(pl.multiple_of(j * UNIT, UNIT), UNIT)
        acc[j] = acc[j] + mm_tn(gs[:, cols], dout[...])
        flush(j)
        acc[4 + j] = acc[4 + j] + mm(mT[...], zs[:, cols])
        flush(4 + j)
        return carry

    lax.fori_loop(0, n_ff, mlp_unit, 0)

    @pl.when(step == last)
    def _():
        for k in range(12):
            pltpu.make_async_copy(acc.at[k], acc_h.at[k], sem.at[k]).wait()


def reduce_kernel(cfg, x_ref, emb_ref, qkv_ref, u_ref, mix_ref, dmid_ref, wo_ref, wq_h, wk_h, wv_h, acc_h,
                  dx_ref, dn_h, up_h, q_h, k_h, v_h, o_h,
                  wqkvT, dqkv, acc2, aw, r1, r2, r3, res, send, recv, lsem, osem, wsem):
    S, D, HW = cfg
    NQ = D // QW
    scale = HW ** -0.5
    step = pl.program_id(0)
    me = lax.axis_index('data')
    core = lax.rem(me, 2)
    bit_x = lax.rem(me // 2, 2)
    bit_y = me // 4
    core_peer = me + 1 - 2 * core
    x_peer = me + 2 - 4 * bit_x
    y_peer = me + 4 - 8 * bit_y
    half = UNIT // 2
    N_EARLY = 8
    N_ALL = 12

    def order(k):
        if k % 2 == 0:
            return (bit_x, x_peer), (bit_y, y_peer)
        return (bit_y, y_peer), (bit_x, x_peer)

    def aligned(v, n):
        return pl.ds(pl.multiple_of(v, n), n)

    def remote(stage, k, src, dst, peer):
        return pltpu.make_async_remote_copy(src_ref=src, dst_ref=dst, send_sem=send.at[stage, k], recv_sem=recv.at[stage, k], device_id=(peer,), device_id_type=MESH)

    def copy_of(stage, k):
        (b1, p1), (b2, p2) = order(k)
        if stage == 0:
            rows = aligned((1 - core) * half, half)
            src = acc_h.at[k, rows] if k < N_EARLY else acc2.at[k - N_EARLY, rows]
            return remote(0, k, src, r1.at[k], core_peer)
        if stage == 1:
            return remote(1, k, aw.at[k, aligned((1 - b1) * 128, 128)], r2.at[k], p1)
        if stage == 2:
            return remote(2, k, aw.at[k, aligned(b1 * 128 + (1 - b2) * 64, 64)], r3.at[k], p2)
        if stage == 3:
            mine = res.at[k, aligned(core * half + b1 * 128 + b2 * 64, 64)]
            return remote(3, k, mine, mine, p2)
        if stage == 4:
            mine = res.at[k, aligned(core * half + b1 * 128, 128)]
            return remote(4, k, mine, mine, p1)
        mine = res.at[k, aligned(core * half, half)]
        return remote(5, k, mine, mine, core_peer)

    def out_copy(k):
        if k < 4:
            dst = dn_h.at[k * UNIT:(k + 1) * UNIT]
        elif k < 8:
            dst = up_h.at[:, (k - 4) * UNIT:(k - 3) * UNIT]
        else:
            dst = (q_h, k_h, v_h, o_h)[k - 8]
        return pltpu.make_async_copy(res.at[k], dst, osem.at[k])

    def own_load(k):
        return pltpu.make_async_copy(acc_h.at[k, aligned(core * half, half)], aw.at[k], lsem.at[k])

    def late_load(k):
        return pltpu.make_async_copy(acc_h.at[k], acc2.at[k - N_EARLY], lsem.at[k])

    def serve(stage, k):
        (b1, _), (b2, _) = order(k)
        if stage == 0:
            if k < N_EARLY:
                own_load(k).wait()
                copy_of(0, k).wait_recv()
                aw[k] = aw[k] + r1[k]
            else:
                copy_of(0, k).wait_recv()
                aw[k] = acc2[k - N_EARLY, aligned(core * half, half)] + r1[k]
        elif stage == 1:
            copy_of(1, k).wait_recv()
            rows = aligned(b1 * 128, 128)
            aw[k, rows] = aw[k, rows] + r2[k]
        elif stage == 2:
            copy_of(2, k).wait_recv()
            res[k, aligned(core * half + b1 * 128 + b2 * 64, 64)] = aw[k, aligned(b1 * 128 + b2 * 64, 64)] + r3[k]
        else:
            copy_of(stage, k).wait_recv()
        if stage < 5:
            copy_of(stage + 1, k).start()
        else:
            out_copy(k).start()

    def at_step(i, events):
        @pl.when(step == i)
        def _():
            for stage, k in events:
                serve(stage, k)

    @pl.when(step == 0)
    def _():
        barrier = pltpu.get_barrier_semaphore()
        for peer in (core_peer, x_peer, y_peer):
            pl.semaphore_signal(barrier, inc=1, device_id=(peer,), device_id_type=MESH)
        loads = [pltpu.make_async_copy(w, wqkvT.at[j * D:(j + 1) * D], wsem.at[j]) for j, w in enumerate((wq_h, wk_h, wv_h))]
        for k in range(N_EARLY):
            own_load(k).start()
        pl.semaphore_wait(barrier, 3)
        for k in range(N_EARLY):
            copy_of(0, k).start()
        for cp in loads:
            cp.start()
        for k in range(N_EARLY, N_ALL):
            late_load(k).start()
        for k in range(4):
            serve(0, k)
        for cp in loads:
            cp.wait()
        for k in range(N_EARLY, N_ALL):
            late_load(k).wait()

    d_mid = dmid_ref[0]
    d_mix = mm_nt(d_mid, wo_ref[...]).astype(BF)
    for c in range(NQ):
        qc = slice(c * QW, (c + 1) * QW)
        kc = slice(D + c * QW, D + (c + 1) * QW)
        vc = slice(2 * D + c * QW, 2 * D + (c + 1) * QW)

        def get_p(qs, k4, cols):
            m, e, inv = soft_stats(mm_nt(k4, qs).astype(BF), scale)
            return e * inv

        dq, dk, dv = attn_bwd_quad(qkv_ref[0, :, qc], qkv_ref[0, :, kc], qkv_ref[0, :, vc], d_mix[:, qc], HW, get_p)
        dqkv[:, qc] = dq
        dqkv[:, kc] = dk
        dqkv[:, vc] = dv
    d_norm_x = mm(dqkv[...], wqkvT[...]).astype(BF)
    x = x_ref[0] + emb_ref[0:1, :]
    dx_ref[0] = d_mid + rms_bwd(x, d_norm_x)

    def attn_unit(j, carry):
        cols = pl.ds(pl.multiple_of(j * UNIT, UNIT), UNIT)
        acc2[j] = acc2[j] + mm_tn(dqkv[:, cols], u_ref[0])
        return carry

    lax.fori_loop(0, 3, attn_unit, 0)
    acc2[3] = acc2[3] + mm(mix_ref[...], d_mid)

    at_step(0, [(0, k) for k in range(4, 8)])
    at_step(1, [(1, 0), (1, 1)])
    at_step(2, [(1, 2), (1, 3)])
    at_step(3, [(1, 4), (1, 5), (2, 0), (2, 1)])
    at_step(4, [(1, 6), (1, 7), (2, 2), (2, 3)])

    @pl.when(step == 5)
    def _():
        for k in range(N_EARLY, N_ALL):
            copy_of(0, k).start()
        plan = [(2, 4), (2, 5), (3, 0), (3, 1), (0, 8), (0, 9), (0, 10), (0, 11), (2, 6), (2, 7), (3, 2), (3, 3),
                (1, 8), (1, 9), (3, 4), (3, 5), (1, 10), (1, 11), (4, 0), (4, 1), (3, 6), (3, 7), (2, 8), (2, 9),
                (4, 2), (4, 3), (5, 0), (5, 1), (2, 10), (2, 11), (4, 4), (4, 5), (5, 2), (5, 3), (3, 8), (3, 9),
                (4, 6), (4, 7), (3, 10), (3, 11), (5, 4), (5, 5), (5, 6), (5, 7), (4, 8), (4, 9), (4, 10), (4, 11),
                (5, 8), (5, 9), (5, 10), (5, 11)]
        for stage, k in plan:
            serve(stage, k)
        for k in range(N_ALL):
            for stage in range(6):
                copy_of(stage, k).wait_send()
        for k in range(N_ALL):
            out_copy(k).wait()


def solution(mesh):
    batch_spec = P('data', None, None)

    def per_device(x, g, emb, w_q, w_k, w_v, w_o, wup, wdn):
        D, H, HW = w_q.shape
        B, S, _ = x.shape
        FF = wup.shape[1]
        L = emb.shape[0]
        T = L * S
        NQ = D // QW
        NS = QW // HW
        w_t = [w.transpose(1, 2, 0).reshape(D, D) for w in (w_q, w_k, w_v)]
        wo = w_o.reshape(D, D)
        const = lambda shape: pl.BlockSpec(shape, lambda b: (0,) * len(shape), pipeline_mode=pl.Buffered(1))
        per_seq = lambda cols: pl.BlockSpec((1, S, cols), lambda b: (b, 0, 0))
        col_seq = pl.BlockSpec((D, S), lambda b: (0, b))
        hbm = pl.BlockSpec(memory_space=pl.ANY)
        sds = jax.ShapeDtypeStruct
        acc, qkv0, u0, mix0, dmid0 = pl.pallas_call(
            functools.partial(step_kernel, (S, D, FF, HW, L)),
            name='block_grads',
            grid=(B,),
            in_specs=[per_seq(D), per_seq(D), const(emb.shape), hbm, hbm, hbm, const(wo.shape), const(wup.shape), const(wdn.shape)],
            out_specs=[hbm, per_seq(3 * D), per_seq(D), col_seq, per_seq(D)],
            out_shape=[sds((12, UNIT, UNIT), F32), sds((B, S, 3 * D), BF), sds((B, S, D), BF), sds((D, B * S), BF), sds((B, S, D), BF)],
            scratch_shapes=[
                pltpu.VMEM((L, S, D), BF),
                pltpu.VMEM((T, D), BF),
                pltpu.VMEM((T, 3 * D), BF),
                pltpu.VMEM((L, NQ, S, NS * S), BF),
                pltpu.VMEM((L, NQ, 8, NS * S), F32),
                pltpu.VMEM((D, T), BF),
                pltpu.VMEM((L, S, D), BF),
                pltpu.VMEM((D, T), BF),
                pltpu.VMEM((T, FF), BF),
                pltpu.VMEM((T, FF), BF),
                pltpu.VMEM((T, D), BF),
                pltpu.VMEM((T, D), BF),
                pltpu.VMEM((S, D), BF),
                pltpu.VMEM((3 * D, D), BF),
                pltpu.VMEM((12, UNIT, UNIT), F32),
                pltpu.SemaphoreType.DMA((12,)),
                pltpu.SemaphoreType.DMA((3,)),
            ],
            compiler_params=pltpu.CompilerParams(dimension_semantics=('arbitrary',), vmem_limit_bytes=VMEM_MAX),
        )(x, g, emb, *w_t, wo, wup, wdn)
        outs = pl.pallas_call(
            functools.partial(reduce_kernel, (S, D, HW)),
            name='attn_reduce',
            grid=(B,),
            in_specs=[per_seq(D), const(emb.shape), per_seq(3 * D), per_seq(D), col_seq, per_seq(D), const(wo.shape), hbm, hbm, hbm, hbm],
            out_specs=[per_seq(D)] + [hbm] * 6,
            out_shape=[sds(x.shape, BF), sds((FF, D), F32), sds((D, FF), F32)] + [sds((D, D), F32)] * 4,
            scratch_shapes=[
                pltpu.VMEM((3 * D, D), BF),
                pltpu.VMEM((S, 3 * D), BF),
                pltpu.VMEM((4, UNIT, UNIT), F32),
                pltpu.VMEM((12, UNIT // 2, UNIT), F32),
                pltpu.VMEM((12, UNIT // 2, UNIT), F32),
                pltpu.VMEM((12, 128, UNIT), F32),
                pltpu.VMEM((12, 64, UNIT), F32),
                pltpu.VMEM((12, UNIT, UNIT), F32),
                pltpu.SemaphoreType.DMA((6, 12)),
                pltpu.SemaphoreType.DMA((6, 12)),
                pltpu.SemaphoreType.DMA((12,)),
                pltpu.SemaphoreType.DMA((12,)),
                pltpu.SemaphoreType.DMA((3,)),
            ],
            compiler_params=pltpu.CompilerParams(dimension_semantics=('arbitrary',), vmem_limit_bytes=VMEM_MAX, collective_id=0, has_side_effects=True),
        )(x, emb, qkv0, u0, mix0, dmid0, wo, *w_t, acc)
        d_x, dn, up, gq, gk, gv, go = outs
        back = lambda a: a.reshape(H, HW, D).transpose(2, 0, 1)
        return back(gq), back(gk), back(gv), go.reshape(H, HW, D), up, dn, d_x

    return jax.shard_map(per_device, mesh=mesh, in_specs=(batch_spec, batch_spec, P(), P(), P(), P(), P(), P(), P()), out_specs=(P(), P(), P(), P(), P(), P(), batch_spec), check_vma=False)
```

time: 535 us -> 425 us (0.79)
  waiting for transfers between devices: 163 us -> 0 us
  Pallas kernels: 334 us -> 411 us
  between operations: 14.1 us -> 0.68 us
  local copies, waits for them, and re-layouts: 22.2 us -> 13.8 us
    psum x1 -> x0, waiting for transfers between devices: 163 us -> none  [per_device(): gqkv, go, gup, gdnT = lax.psum((gqkv, go, gup, gdnT), 'data')]
    pallas_call x1 -> x2, Pallas kernels: 334 us -> 411 us  [the longest x1 283 us: per_device(): pl.pallas_call(functools.partial(step_kernel, (S, D, FF, HW, L)), name='b...]
    slice x4 -> x0, local copies, waits for them, and re-layouts: 6.09 us -> none  [per_device(): gqkv[:, i * H * HW:(i + 1) * H * HW].reshape(D, H, HW)]
    unnamed x5 -> x19, local copies, waits for them, and re-layouts: 11.1 us -> 13.8 us
  transfers between devices with their start and end apart: 1 -> 0, of which waited for: 1 -> 0; matrix products, arithmetic and copies ran while one was open for 0% -> 0% of each run, Pallas kernels for 0% -> 0%
where the time goes in v2:
time: 425 us
  Pallas kernels  411 us (97%)
  local copies, waits for them, and re-layouts  13.8 us (3%)
    pallas_call x1, Pallas kernels, per_device(): pl.pallas_call(functools.partial(step_kernel, (S, D, FF, HW, L)), name='b...  283 us
    pallas_call x1, Pallas kernels, per_device(): pl.pallas_call(functools.partial(reduce_kernel, (S, D, HW)), name='attn_r...  127 us
    unnamed x19, local copies, waits for them, and re-layouts  13.8 us

profile of v2, /device:TPU:0, one launch (start us, length us, event | category | flops | bytes accessed | tf_op | source)
XLA Modules:
  0.0 425.0 jit_solution(18386086764915537321)
XLA Ops:
  0.6 283.4 %block_grads.1 = (f32[12,512,512]{2,1,0:T(8,128)}, bf16[6,384,1536]{2,1,0:T(8,128)(2,1)}, bf16[6,384,512]{2,1,0:T(8,128)(2,1)}, bf16[512,2304]{1,0:T(8,128)(2,1)}, bf16[6,384,512]{2,1,0:T(8,128)(2,1)}) custom-call(bf16[6,384,512]{2,1,0:T(8,128)(2,1)} %x_ref.3, bf16[6,384,512]{2,1,0:T(8,128)(2,1)} %g_ref.1, bf16[3,512]{1,0:T(4,128)(2,1)} %emb_ref.3, ...), custom_call_target="tpu_custom_call" | custom-call | tf_op jit(solution)/shard_map/block_grads/pallas_call | solution.py:428
  284.0 127.2 %attn_reduce.1 = (bf16[6,384,512]{2,1,0:T(8,128)(2,1)}, f32[2048,512]{1,0:T(8,128)}, f32[512,2048]{1,0:T(8,128)}, f32[512,512]{1,0:T(8,128)}, f32[512,512]{1,0:T...) custom-call(bf16[6,384,512]{2,1,0:T(8,128)(2,1)} %x_ref.3, bf16[3,512]{1,0:T(4,128)(2,1)} %emb_ref.3, ...), custom_call_target="tpu_custom_call" | custom-call | tf_op jit(solution)/shard_map/attn_reduce/pallas_call | solution.py:456
  411.2 0.0 copy-start.5
  411.2 0.0 copy-start.4
  411.2 0.0 copy-start.3
  411.2 2.4 copy.23
  413.6 0.0 copy-done.5
  413.6 0.0 copy-start.1
  413.7 1.0 copy.24
  414.6 0.0 copy-done.4
  414.6 1.0 copy.25
  415.6 0.0 copy-done.3
  415.6 1.0 copy.26
  416.6 0.2 copy-done.1
  416.7 0.0 copy-start
  416.7 2.1 copy.27
  418.9 1.6 copy-done
  420.4 0.0 copy-start.2
  420.4 2.1 copy.28
  422.6 1.0 copy-done.2
  423.6 1.4 copy.29
Async XLA Ops:
  411.2 2.4 copy-start.5
  411.2 3.4 copy-start.4
  411.2 4.4 %copy-start.3 = (f32[512,512]{1,0:T(8,128)S(1)}, f32[512,512]{1,0:T(8,128)}, u32[]{:S(2)}) copy-start(f32[512,512]{1,0:T(8,128)} %get-tuple-element.27) | copy-start | bytes 3145732
  413.6 3.1 copy-start.1
  416.7 3.7 copy-start
  420.4 3.2 copy-start.2

commit v3 on v2

--- a/solution.py
+++ b/solution.py
@@ -54,7 +54,7 @@
     zf = z.astype(F32)
     z2 = zf * zf
     t = jnp.tanh(zf * (GELU_C + (GELU_C * GELU_A) * z2))
-    slope = (0.5 + 0.5 * t) + (1.0 - t * t) * (zf * ((0.5 * GELU_C) + (1.5 * GELU_C * GELU_A) * z2))
+    slope = (0.5 + 0.5 * t) + ((1.0 - t * t) * zf) * ((0.5 * GELU_C) + (1.5 * GELU_C * GELU_A) * z2)
     return (dg.astype(F32) * slope).astype(BF)
 
 
@@ -99,8 +99,8 @@
 
 
 def step_kernel(cfg, x_ref, g_ref, emb_ref, wq_h, wk_h, wv_h, wo_ref, wup_ref, wdn_ref,
-                acc_h, qkv0_ref, u0_ref, mix0_ref, dmid0_ref,
-                xs, us, qkv, st, stat, mixT, hs, mT, zs, gs, dmid, dout, dcur, wqkvT, acc, sem, wsem):
+                acc_h, qkv0_h, u0_h, mix0_h, z0_h, mT0_h, h0_h, dout0_h,
+                xs, us, qkv, st, stat, mixT, hs, mT, zs, gs, dmid, dout, dcur, wqkvT, acc, sem, wsem, ssem):
     S, D, FF, HW, L = cfg
     NQ = D // QW
     NS = QW // HW
@@ -170,9 +170,11 @@
 
     lax.fori_loop(0, L, fwd, 0)
     dcur[...] = g_ref[0]
-    qkv0_ref[0] = qkv[0:S, :]
-    u0_ref[0] = us[0:S, :]
-    mix0_ref[...] = mixT[:, 0:S]
+    saves = [pltpu.make_async_copy(src, dst.at[step], ssem.at[n]) for n, (src, dst) in enumerate((
+        (qkv.at[0:S], qkv0_h), (us.at[0:S], u0_h), (mixT.at[:, 0:S], mix0_h), (zs.at[0:S], z0_h),
+        (mT.at[:, 0:S], mT0_h), (hs.at[0], h0_h), (dout.at[0:S], dout0_h)))]
+    for cp in saves[:-1]:
+        cp.start()
 
     def bwd(i, carry):
         l = L - 1 - i
@@ -186,29 +188,28 @@
         d_norm = mm_nt(zs[rows, :], wup_ref[...]).astype(BF)
         dmid[rows, :] = d_out + rms_bwd(hs[l], d_norm)
 
-        @pl.when(l > 0)
-        def _():
-            d_mid = dmid[rows, :]
-            d_mix = mm_nt(d_mid, wo_ref[...]).astype(BF)
-            for c in range(NQ):
-                qc = slice(c * QW, (c + 1) * QW)
-                kc = slice(D + c * QW, D + (c + 1) * QW)
-                vc = slice(2 * D + c * QW, 2 * D + (c + 1) * QW)
-
-                def get_p(qs, k4, cols):
-                    s = st[l, c, :, cols].astype(F32)
-                    return jnp.exp2((s - stat[l, c, 0:1, cols]) * (scale * LOG2E)) * stat[l, c, 1:2, cols]
-
-                dq, dk, dv = attn_bwd_quad(qkv[rows, qc], qkv[rows, kc], qkv[rows, vc], d_mix[:, qc], HW, get_p)
-                qkv[rows, qc] = dq
-                qkv[rows, kc] = dk
-                qkv[rows, vc] = dv
-            d_norm_x = mm(qkv[rows, :], wqkvT[...]).astype(BF)
-            dcur[...] = d_mid + rms_bwd(xs[l], d_norm_x)
+        d_mid = dmid[rows, :]
+        d_mix = mm_nt(d_mid, wo_ref[...]).astype(BF)
+        for c in range(NQ):
+            qc = slice(c * QW, (c + 1) * QW)
+            kc = slice(D + c * QW, D + (c + 1) * QW)
+            vc = slice(2 * D + c * QW, 2 * D + (c + 1) * QW)
+
+            def get_p(qs, k4, cols):
+                s = st[l, c, :, cols].astype(F32)
+                return jnp.exp2((s - stat[l, c, 0:1, cols]) * (scale * LOG2E)) * stat[l, c, 1:2, cols]
+
+            dq, dk, dv = attn_bwd_quad(qkv[rows, qc], qkv[rows, kc], qkv[rows, vc], d_mix[:, qc], HW, get_p)
+            qkv[rows, qc] = dq
+            qkv[rows, kc] = dk
+            qkv[rows, vc] = dv
+        d_norm_x = mm(qkv[rows, :], wqkvT[...]).astype(BF)
+        dcur[...] = d_mid + rms_bwd(xs[l], d_norm_x)
         return carry
 
-    lax.fori_loop(0, L, bwd, 0)
-    dmid0_ref[0] = dmid[0:S, :]
+    lax.fori_loop(0, L - 1, bwd, 0)
+    dout[0:S, :] = dcur[...]
+    saves[-1].start()
 
     def flush(k):
         @pl.when(step == last)
@@ -229,11 +230,13 @@
         cols = pl.ds(pl.multiple_of(j * UNIT, UNIT), UNIT)
         acc[j] = acc[j] + mm_tn(gs[:, cols], dout[...])
         flush(j)
-        acc[4 + j] = acc[4 + j] + mm(mT[...], zs[:, cols])
+        acc[4 + j] = acc[4 + j] + mm(mT[:, S:], zs[S:, cols])
         flush(4 + j)
         return carry
 
     lax.fori_loop(0, n_ff, mlp_unit, 0)
+    for cp in saves:
+        cp.wait()
 
     @pl.when(step == last)
     def _():
@@ -241,11 +244,12 @@
             pltpu.make_async_copy(acc.at[k], acc_h.at[k], sem.at[k]).wait()
 
 
-def reduce_kernel(cfg, x_ref, emb_ref, qkv_ref, u_ref, mix_ref, dmid_ref, wo_ref, wq_h, wk_h, wv_h, acc_h,
+def reduce_kernel(cfg, x_ref, emb_ref, qkv_ref, u_ref, mix_ref, z_ref, mT_ref, h_ref, dout_ref, wo_ref, wq_h, wk_h, wv_h, wup_h, wdn_h, acc_h,
                   dx_ref, dn_h, up_h, q_h, k_h, v_h, o_h,
-                  wqkvT, dqkv, acc2, aw, r1, r2, r3, res, send, recv, lsem, osem, wsem):
-    S, D, HW = cfg
+                  wqkvT, wup, wdn, dup, dmid, dqkv, acc2, aw, r1, r2, r3, res, send, recv, lsem, osem, wsem):
+    B, S, D, FF, HW = cfg
     NQ = D // QW
+    n_ff = FF // UNIT
     scale = HW ** -0.5
     step = pl.program_id(0)
     me = lax.axis_index('data')
@@ -256,7 +260,7 @@
     x_peer = me + 2 - 4 * bit_x
     y_peer = me + 4 - 8 * bit_y
     half = UNIT // 2
-    N_EARLY = 8
+    N_EARLY = n_ff
     N_ALL = 12
 
     def order(k):
@@ -266,6 +270,11 @@
 
     def aligned(v, n):
         return pl.ds(pl.multiple_of(v, n), n)
+
+    def part(k, start, n):
+        if k < N_EARLY:
+            return aw.at[k, aligned(start, n)]
+        return acc2.at[k - N_EARLY, aligned(core * half + start, n)]
 
     def remote(stage, k, src, dst, peer):
         return pltpu.make_async_remote_copy(src_ref=src, dst_ref=dst, send_sem=send.at[stage, k], recv_sem=recv.at[stage, k], device_id=(peer,), device_id_type=MESH)
@@ -277,9 +286,9 @@
             src = acc_h.at[k, rows] if k < N_EARLY else acc2.at[k - N_EARLY, rows]
             return remote(0, k, src, r1.at[k], core_peer)
         if stage == 1:
-            return remote(1, k, aw.at[k, aligned((1 - b1) * 128, 128)], r2.at[k], p1)
+            return remote(1, k, part(k, (1 - b1) * 128, 128), r2.at[k], p1)
         if stage == 2:
-            return remote(2, k, aw.at[k, aligned(b1 * 128 + (1 - b2) * 64, 64)], r3.at[k], p2)
+            return remote(2, k, part(k, b1 * 128 + (1 - b2) * 64, 64), r3.at[k], p2)
         if stage == 3:
             mine = res.at[k, aligned(core * half + b1 * 128 + b2 * 64, 64)]
             return remote(3, k, mine, mine, p2)
@@ -306,98 +315,119 @@
 
     def serve(stage, k):
         (b1, _), (b2, _) = order(k)
+        copy_of(stage, k).wait_recv()
         if stage == 0:
             if k < N_EARLY:
                 own_load(k).wait()
-                copy_of(0, k).wait_recv()
-                aw[k] = aw[k] + r1[k]
-            else:
-                copy_of(0, k).wait_recv()
-                aw[k] = acc2[k - N_EARLY, aligned(core * half, half)] + r1[k]
+            ref = part(k, 0, half)
+            ref[...] = ref[...] + r1[k]
         elif stage == 1:
-            copy_of(1, k).wait_recv()
-            rows = aligned(b1 * 128, 128)
-            aw[k, rows] = aw[k, rows] + r2[k]
+            ref = part(k, b1 * 128, 128)
+            ref[...] = ref[...] + r2[k]
         elif stage == 2:
-            copy_of(2, k).wait_recv()
-            res[k, aligned(core * half + b1 * 128 + b2 * 64, 64)] = aw[k, aligned(b1 * 128 + b2 * 64, 64)] + r3[k]
-        else:
-            copy_of(stage, k).wait_recv()
+            ref = part(k, b1 * 128 + b2 * 64, 64)
+            res[k, aligned(core * half + b1 * 128 + b2 * 64, 64)] = ref[...] + r3[k]
         if stage < 5:
             copy_of(stage + 1, k).start()
         else:
             out_copy(k).start()
 
-    def at_step(i, events):
-        @pl.when(step == i)
-        def _():
-            for stage, k in events:
-                serve(stage, k)
+    def serve_all(stage, units):
+        for k in units:
+            serve(stage, k)
+
+    def begin(units):
+        for k in units:
+            copy_of(0, k).start()
+
+    def w_loads():
+        pairs = [(wdn_h, wdn), (wup_h, wup)] + [(w, wqkvT.at[j * D:(j + 1) * D]) for j, w in enumerate((wq_h, wk_h, wv_h))]
+        return [pltpu.make_async_copy(s_, d_, wsem.at[j]) for j, (s_, d_) in enumerate(pairs)]
 
     @pl.when(step == 0)
     def _():
         barrier = pltpu.get_barrier_semaphore()
         for peer in (core_peer, x_peer, y_peer):
             pl.semaphore_signal(barrier, inc=1, device_id=(peer,), device_id_type=MESH)
-        loads = [pltpu.make_async_copy(w, wqkvT.at[j * D:(j + 1) * D], wsem.at[j]) for j, w in enumerate((wq_h, wk_h, wv_h))]
         for k in range(N_EARLY):
             own_load(k).start()
+        for cp in w_loads():
+            cp.start()
         pl.semaphore_wait(barrier, 3)
-        for k in range(N_EARLY):
-            copy_of(0, k).start()
-        for cp in loads:
-            cp.start()
+        begin(range(N_EARLY))
         for k in range(N_EARLY, N_ALL):
             late_load(k).start()
-        for k in range(4):
-            serve(0, k)
-        for cp in loads:
+        serve_all(0, range(N_EARLY))
+        for cp in w_loads():
             cp.wait()
         for k in range(N_EARLY, N_ALL):
             late_load(k).wait()
 
-    d_mid = dmid_ref[0]
-    d_mix = mm_nt(d_mid, wo_ref[...]).astype(BF)
-    for c in range(NQ):
-        qc = slice(c * QW, (c + 1) * QW)
-        kc = slice(D + c * QW, D + (c + 1) * QW)
-        vc = slice(2 * D + c * QW, 2 * D + (c + 1) * QW)
-
-        def get_p(qs, k4, cols):
-            m, e, inv = soft_stats(mm_nt(k4, qs).astype(BF), scale)
-            return e * inv
-
-        dq, dk, dv = attn_bwd_quad(qkv_ref[0, :, qc], qkv_ref[0, :, kc], qkv_ref[0, :, vc], d_mix[:, qc], HW, get_p)
-        dqkv[:, qc] = dq
-        dqkv[:, kc] = dk
-        dqkv[:, vc] = dv
-    d_norm_x = mm(dqkv[...], wqkvT[...]).astype(BF)
-    x = x_ref[0] + emb_ref[0:1, :]
-    dx_ref[0] = d_mid + rms_bwd(x, d_norm_x)
-
-    def attn_unit(j, carry):
-        cols = pl.ds(pl.multiple_of(j * UNIT, UNIT), UNIT)
-        acc2[j] = acc2[j] + mm_tn(dqkv[:, cols], u_ref[0])
-        return carry
-
-    lax.fori_loop(0, 3, attn_unit, 0)
-    acc2[3] = acc2[3] + mm(mix_ref[...], d_mid)
-
-    at_step(0, [(0, k) for k in range(4, 8)])
+    @pl.when(step < B)
+    def _():
+        d_out = dout_ref[0]
+        for j in range(n_ff):
+            cols = slice(j * UNIT, (j + 1) * UNIT)
+            d_act = mm_nt(d_out, wdn[cols, :]).astype(BF)
+            dup[:, cols] = gelu_bwd(z_ref[0, :, cols], d_act)
+        d_norm = mm_nt(dup[...], wup[...]).astype(BF)
+        d_mid = d_out + rms_bwd(h_ref[0], d_norm)
+        dmid[step] = d_mid
+        for j in range(n_ff):
+            acc2[j] = acc2[j] + mm(mT_ref[0], dup[:, j * UNIT:(j + 1) * UNIT])
+        acc2[7] = acc2[7] + mm(mix_ref[0], d_mid)
+
+    @pl.when(step >= B)
+    def _():
+        d_mid = dmid[step - B]
+        d_mix = mm_nt(d_mid, wo_ref[...]).astype(BF)
+        for c in range(NQ):
+            qc = slice(c * QW, (c + 1) * QW)
+            kc = slice(D + c * QW, D + (c + 1) * QW)
+            vc = slice(2 * D + c * QW, 2 * D + (c + 1) * QW)
+
+            def get_p(qs, k4, cols):
+                m, e, inv = soft_stats(mm_nt(k4, qs).astype(BF), scale)
+                return e * inv
+
+            dq, dk, dv = attn_bwd_quad(qkv_ref[0, :, qc], qkv_ref[0, :, kc], qkv_ref[0, :, vc], d_mix[:, qc], HW, get_p)
+            dqkv[:, qc] = dq
+            dqkv[:, kc] = dk
+            dqkv[:, vc] = dv
+        d_norm_x = mm(dqkv[...], wqkvT[...]).astype(BF)
+        x = x_ref[0] + emb_ref[0:1, :]
+        dx_ref[0] = d_mid + rms_bwd(x, d_norm_x)
+
+        def attn_unit(j, carry):
+            cols = pl.ds(pl.multiple_of(j * UNIT, UNIT), UNIT)
+            acc2[4 + j] = acc2[4 + j] + mm_tn(dqkv[:, cols], u_ref[0])
+            return carry
+
+        lax.fori_loop(0, 3, attn_unit, 0)
+
+    def at_step(i, events, before=None):
+        @pl.when(step == i)
+        def _():
+            if before is not None:
+                begin(before)
+            for stage, k in events:
+                serve(stage, k)
+
     at_step(1, [(1, 0), (1, 1)])
-    at_step(2, [(1, 2), (1, 3)])
-    at_step(3, [(1, 4), (1, 5), (2, 0), (2, 1)])
-    at_step(4, [(1, 6), (1, 7), (2, 2), (2, 3)])
-
-    @pl.when(step == 5)
+    at_step(3, [(1, 2), (1, 3)])
+    at_step(4, [(2, 0), (2, 1)])
+    at_step(5, [(2, 2), (2, 3), (0, 4), (0, 5), (0, 6), (0, 7), (0, 11), (3, 0), (3, 1)], before=[4, 5, 6, 7, 11])
+    at_step(6, [(3, 2), (3, 3), (1, 4), (1, 5)])
+    at_step(7, [(4, 0), (4, 1), (1, 6), (1, 7)])
+    at_step(8, [(4, 2), (4, 3), (1, 11), (2, 4), (2, 5)])
+    at_step(9, [(5, 0), (5, 1), (5, 2), (5, 3), (2, 6), (2, 7), (3, 4), (3, 5)])
+    at_step(10, [(2, 11), (3, 6), (3, 7), (4, 4), (4, 5)])
+
+    @pl.when(step == 2 * B - 1)
     def _():
-        for k in range(N_EARLY, N_ALL):
-            copy_of(0, k).start()
-        plan = [(2, 4), (2, 5), (3, 0), (3, 1), (0, 8), (0, 9), (0, 10), (0, 11), (2, 6), (2, 7), (3, 2), (3, 3),
-                (1, 8), (1, 9), (3, 4), (3, 5), (1, 10), (1, 11), (4, 0), (4, 1), (3, 6), (3, 7), (2, 8), (2, 9),
-                (4, 2), (4, 3), (5, 0), (5, 1), (2, 10), (2, 11), (4, 4), (4, 5), (5, 2), (5, 3), (3, 8), (3, 9),
-                (4, 6), (4, 7), (3, 10), (3, 11), (5, 4), (5, 5), (5, 6), (5, 7), (4, 8), (4, 9), (4, 10), (4, 11),
-                (5, 8), (5, 9), (5, 10), (5, 11)]
+        begin([8, 9, 10])
+        plan = [(4, 6), (4, 7), (0, 8), (0, 9), (0, 10), (3, 11), (5, 4), (5, 5), (1, 8), (1, 9), (4, 11), (5, 6), (5, 7),
+                (1, 10), (2, 8), (2, 9), (5, 11), (2, 10), (3, 8), (3, 9), (3, 10), (4, 8), (4, 9), (4, 10), (5, 8), (5, 9), (5, 10)]
         for stage, k in plan:
             serve(stage, k)
         for k in range(N_ALL):
@@ -425,13 +455,14 @@
         col_seq = pl.BlockSpec((D, S), lambda b: (0, b))
         hbm = pl.BlockSpec(memory_space=pl.ANY)
         sds = jax.ShapeDtypeStruct
-        acc, qkv0, u0, mix0, dmid0 = pl.pallas_call(
+        saved = [sds((B, S, 3 * D), BF), sds((B, S, D), BF), sds((B, D, S), BF), sds((B, S, FF), BF), sds((B, D, S), BF), sds((B, S, D), BF), sds((B, S, D), BF)]
+        acc, qkv0, u0, mix0, z0, mT0, h0, dout0 = pl.pallas_call(
             functools.partial(step_kernel, (S, D, FF, HW, L)),
             name='block_grads',
             grid=(B,),
             in_specs=[per_seq(D), per_seq(D), const(emb.shape), hbm, hbm, hbm, const(wo.shape), const(wup.shape), const(wdn.shape)],
-            out_specs=[hbm, per_seq(3 * D), per_seq(D), col_seq, per_seq(D)],
-            out_shape=[sds((12, UNIT, UNIT), F32), sds((B, S, 3 * D), BF), sds((B, S, D), BF), sds((D, B * S), BF), sds((B, S, D), BF)],
+            out_specs=[hbm] * 8,
+            out_shape=[sds((12, UNIT, UNIT), F32)] + saved,
             scratch_shapes=[
                 pltpu.VMEM((L, S, D), BF),
                 pltpu.VMEM((T, D), BF),
@@ -450,21 +481,28 @@
                 pltpu.VMEM((12, UNIT, UNIT), F32),
                 pltpu.SemaphoreType.DMA((12,)),
                 pltpu.SemaphoreType.DMA((3,)),
+                pltpu.SemaphoreType.DMA((7,)),
             ],
             compiler_params=pltpu.CompilerParams(dimension_semantics=('arbitrary',), vmem_limit_bytes=VMEM_MAX),
         )(x, g, emb, *w_t, wo, wup, wdn)
+        first = lambda *shape: pl.BlockSpec((1,) + shape, lambda i: (jnp.minimum(i, B - 1), 0, 0))
+        second = lambda *shape: pl.BlockSpec((1,) + shape, lambda i: (jnp.maximum(i - B, 0), 0, 0))
         outs = pl.pallas_call(
-            functools.partial(reduce_kernel, (S, D, HW)),
+            functools.partial(reduce_kernel, (B, S, D, FF, HW)),
             name='attn_reduce',
-            grid=(B,),
-            in_specs=[per_seq(D), const(emb.shape), per_seq(3 * D), per_seq(D), col_seq, per_seq(D), const(wo.shape), hbm, hbm, hbm, hbm],
-            out_specs=[per_seq(D)] + [hbm] * 6,
+            grid=(2 * B,),
+            in_specs=[second(S, D), const(emb.shape), second(S, 3 * D), second(S, D), first(D, S), first(S, FF), first(D, S), first(S, D), first(S, D), const(wo.shape)] + [hbm] * 6,
+            out_specs=[second(S, D)] + [hbm] * 6,
             out_shape=[sds(x.shape, BF), sds((FF, D), F32), sds((D, FF), F32)] + [sds((D, D), F32)] * 4,
             scratch_shapes=[
                 pltpu.VMEM((3 * D, D), BF),
+                pltpu.VMEM((D, FF), BF),
+                pltpu.VMEM((FF, D), BF),
+                pltpu.VMEM((S, FF), BF),
+                pltpu.VMEM((B, S, D), BF),
                 pltpu.VMEM((S, 3 * D), BF),
-                pltpu.VMEM((4, UNIT, UNIT), F32),
-                pltpu.VMEM((12, UNIT // 2, UNIT), F32),
+                pltpu.VMEM((8, UNIT, UNIT), F32),
+                pltpu.VMEM((4, UNIT // 2, UNIT), F32),
                 pltpu.VMEM((12, UNIT // 2, UNIT), F32),
                 pltpu.VMEM((12, 128, UNIT), F32),
                 pltpu.VMEM((12, 64, UNIT), F32),
@@ -473,10 +511,10 @@
                 pltpu.SemaphoreType.DMA((6, 12)),
                 pltpu.SemaphoreType.DMA((12,)),
                 pltpu.SemaphoreType.DMA((12,)),
-                pltpu.SemaphoreType.DMA((3,)),
+                pltpu.SemaphoreType.DMA((5,)),
             ],
             compiler_params=pltpu.CompilerParams(dimension_semantics=('arbitrary',), vmem_limit_bytes=VMEM_MAX, collective_id=0, has_side_effects=True),
-        )(x, emb, qkv0, u0, mix0, dmid0, wo, *w_t, acc)
+        )(x, emb, qkv0, u0, mix0, z0, mT0, h0, dout0, wo, *w_t, wup, wdn, acc)
         d_x, dn, up, gq, gk, gv, go = outs
         back = lambda a: a.reshape(H, HW, D).transpose(2, 0, 1)
         return back(gq), back(gk), back(gv), go.reshape(H, HW, D), up, dn, d_x

time: 425 us -> 409 us (0.962)
  Pallas kernels: 411 us -> 394 us
    pallas_call x1, Pallas kernels: 283 us -> 255 us  [per_device(): pl.pallas_call(functools.partial(step_kernel, (S, D, FF, HW, L)), name='b...]
    pallas_call x1, Pallas kernels: 127 us -> 138 us  [per_device(): pl.pallas_call(functools.partial(reduce_kernel, (B, S, D, FF, HW)), name=...]
where the time goes in v3:
time: 409 us; the launch traced here: 408 us
  Pallas kernels  394 us (96%)
  local copies, waits for them, and re-layouts  13.8 us (3%)
    pallas_call x1, Pallas kernels, per_device(): pl.pallas_call(functools.partial(step_kernel, (S, D, FF, HW, L)), name='b...  255 us
    pallas_call x1, Pallas kernels, per_device(): pl.pallas_call(functools.partial(reduce_kernel, (B, S, D, FF, HW)), name=...  138 us
    unnamed x19, local copies, waits for them, and re-layouts  13.8 us

profile of v3, /device:TPU:0, one launch (start us, length us, event | category | flops | bytes accessed | tf_op | source)
XLA Modules:
  0.0 408.3 jit_solution(10643412565498700001)
XLA Ops:
  0.6 255.5 %block_grads.1 = (f32[12,512,512]{2,1,0:T(8,128)}, bf16[6,384,1536]{2,1,0:T(8,128)(2,1)}, bf16[6,384,512]{2,1,0:T(8,128)(2,1)}, bf16[6,512,384]{2,1,0:T(8,128)(2...) custom-call(bf16[6,384,512]{2,1,0:T(8,128)(2,1)} %x_ref.3, ...), custom_call_target="tpu_custom_call" | custom-call | tf_op jit(solution)/shard_map/block_grads/pallas_call | solution.py:459
  256.1 138.4 %attn_reduce.1 = (bf16[6,384,512]{2,1,0:T(8,128)(2,1)}, f32[2048,512]{1,0:T(8,128)}, f32[512,2048]{1,0:T(8,128)}, f32[512,512]{1,0:T(8,128)}, f32[512,512]{1,0:T...) custom-call(bf16[6,384,512]{2,1,0:T(8,128)(2,1)} %x_ref.3, bf16[3,512]{1,0:T(4,128)(2,1)} %emb_ref.3, ...), custom_call_target="tpu_custom_call" | custom-call | tf_op jit(solution)/shard_map/attn_reduce/pallas_call | solution.py:490
  394.5 0.0 copy-start.5
  394.5 0.0 copy-start.4
  394.5 0.0 copy-start.3
  394.6 2.4 copy.23
  397.0 0.0 copy-done.5
  397.0 0.0 copy-start.1
  397.0 1.0 copy.24
  397.9 0.0 copy-done.4
  397.9 1.0 copy.25
  398.9 0.0 copy-done.3
  398.9 1.0 copy.26
  399.9 0.2 copy-done.1
  400.1 0.0 copy-start
  400.1 2.1 copy.27
  402.2 1.6 copy-done
  403.8 0.0 copy-start.2
  403.8 2.1 copy.28
  405.9 1.0 copy-done.2
  406.9 1.4 copy.29
Async XLA Ops:
  394.5 2.4 copy-start.5
  394.5 3.4 copy-start.4
  394.5 4.4 %copy-start.3 = (f32[512,512]{1,0:T(8,128)S(1)}, f32[512,512]{1,0:T(8,128)}, u32[]{:S(2)}) copy-start(f32[512,512]{1,0:T(8,128)} %get-tuple-element.33) | copy-start | bytes 3145732
  397.0 3.1 copy-start.1
  400.1 3.7 copy-start
  403.8 3.2 copy-start.2
